TPU v7x, 256 devices: a whole 4x4x8 slice. The times are simulated.
256 devices in a mesh: site: 32 (over x_hi, z, core), sec: 8 (over y, x_lo).
Axes of the slice: x: 4 (x_hi: 2, x_lo: 2; x = x_hi * 2 + x_lo), y: 4, z: 8, core: 2. Of those that a mesh axis runs over, the one named last changes fastest.
Arguments:
- left_canon: bfloat16 [32, 4, 16, 128, 128], P('site', None, 'sec'), may hold values from -1.5 to 1.5
- right_canon: bfloat16 [32, 4, 16, 128, 128], P('site', None, 'sec'), may hold values from -1.5 to 1.5
- center_site: bfloat16 [32, 4, 16, 128, 128], P('site', None, 'sec'), may hold values from -6 to 6
- center_bond: bfloat16 [32, 16, 128, 128], P('site', 'sec'), may hold values from -2 to 3
- left_seed: bfloat16 [32, 16, 128, 128], P('site', 'sec'), may hold values from -2 to 4
- right_seed: bfloat16 [32, 16, 128, 128], P('site', 'sec'), may hold values from -2 to 4
- left_sector: int32 [32, 4, 16], P('site'), may hold values from 0 to 15, each once within a row
- onsite: float32 [32, 4], P('site'), may hold values from 0.5 to 2
- bond_shift: float32 [32], P('site'), may hold values from 0.5 to 2
Outputs:
- left_new: bfloat16 [32, 4, 16, 128, 128], P('site', None, 'sec')
- right_new: bfloat16 [32, 4, 16, 128, 128], P('site', None, 'sec')
Inputs may be any that keep to these rules, and one draw needn't show every extreme that they name: `left_sector`: for each site and local state the 16 entries are a permutation of the sectors.
All inputs are finite; a program needn't handle non-finite values.
Results may differ from a plain program's by a relative error of at most 0.028.
Values may be sent and summed in bfloat16 or wider, within the bound.
A program may use at most 64 MiB of HBM per device.

v0:
```python
import jax
import jax.numpy as jnp
from jax import lax
from jax.sharding import PartitionSpec as P

NSI = 10
NAPP = 2


def from_behind(block, axis, distance):
    devices = range(lax.axis_size(axis))
    route = [((i - distance) % len(devices), i) for i in devices]
    return lax.ppermute(block, axis, route)


def in_blocks(array, dim, length):
    lengths = array.shape
    blocks = array.reshape(*lengths[:dim], length, lengths[dim] // length, *lengths[dim + 1 :])
    return jnp.moveaxis(blocks, dim, 0)


def sent_and_summed(array, axis, dim):
    length = lax.axis_size(axis)
    blocks = lax.all_to_all(in_blocks(array, dim, length), axis, 0, 0, tiled=True)
    return jnp.sum(blocks, axis=0)


def in_order(blocks, dim):
    blocks = jnp.moveaxis(blocks, 0, dim)
    lengths = blocks.shape
    return blocks.reshape(*lengths[:dim], lengths[dim] * lengths[dim + 1], *lengths[dim + 2 :])


def from_everyone(array, axis):
    copies = jnp.broadcast_to(array, (lax.axis_size(axis), *array.shape))
    return lax.all_to_all(copies, axis, split_axis=0, concat_axis=0, tiled=True)


def collect(array, axis, dim):
    return in_order(from_everyone(array, axis), dim)


def inverse_root(gram_mat):
    scaling = jnp.sqrt(jnp.sum(gram_mat * gram_mat, axis=(-2, -1), keepdims=True))
    identity = jnp.eye(gram_mat.shape[-1], dtype=jnp.float32)
    upper_part = gram_mat / scaling
    lower_part = jnp.broadcast_to(identity, gram_mat.shape)
    for repeat in range(NSI):
        middle = 1.5 * identity - 0.5 * jnp.matmul(
            lower_part, upper_part, precision=lax.Precision.HIGHEST
        )
        upper_part = jnp.matmul(upper_part, middle, precision=lax.Precision.HIGHEST)
        lower_part = jnp.matmul(middle, lower_part, precision=lax.Precision.HIGHEST)
    return lower_part / jnp.sqrt(scaling)


def trace_sum(blocks):
    return jnp.sum(jnp.diagonal(blocks.astype(jnp.float32), axis1=1, axis2=2))


def left_turn(hold_full, tensor_blocks, indices):
    running = jnp.zeros(tensor_blocks.shape[1:], jnp.float32)
    for physical in range(tensor_blocks.shape[0]):
        chosen = jnp.take(hold_full, indices[physical], axis=0)
        product = jnp.einsum(
            "kab,kbc->kac", chosen, tensor_blocks[physical], preferred_element_type=jnp.float32
        ).astype(jnp.bfloat16)
        running = running + jnp.einsum(
            "kba,kbc->kac", tensor_blocks[physical], product, preferred_element_type=jnp.float32
        )
    return running.astype(jnp.bfloat16)


def right_turn(hold_full, tensor_all, indices):
    running = jnp.zeros((indices.shape[1],) + hold_full.shape[1:], jnp.float32)
    for physical in range(tensor_all.shape[0]):
        picked = jnp.take(tensor_all[physical], indices[physical], axis=0)
        env_chosen = jnp.take(hold_full, indices[physical], axis=0)
        product = jnp.einsum(
            "kab,kbc->kac", picked, env_chosen, preferred_element_type=jnp.float32
        ).astype(jnp.bfloat16)
        running = running + jnp.einsum(
            "kac,kdc->kad", product, picked, preferred_element_type=jnp.float32
        )
    return running.astype(jnp.bfloat16)


def right_polar(gram_right, previous):
    gram_prev = jnp.einsum("kab,kcb->kac", previous, previous, preferred_element_type=jnp.float32)
    unit_right = jnp.matmul(
        inverse_root(gram_prev), previous.astype(jnp.float32), precision=lax.Precision.HIGHEST
    )
    return jnp.matmul(
        jnp.swapaxes(unit_right, -1, -2), inverse_root(gram_right), precision=lax.Precision.HIGHEST
    ).astype(jnp.bfloat16)


def per_device(
    left_canon,
    right_canon,
    center_site,
    center_bond,
    left_seed,
    right_seed,
    left_sector,
    onsite,
    bond_shift,
):
    canon_left = left_canon[0]
    canon_right = right_canon[0]
    site_now = center_site[0]
    bond_now = center_bond[0]
    sources = left_sector[0]
    energy = onsite[0]
    bond_add = bond_shift[0]
    owned = canon_left.shape[1]
    width = canon_left.shape[2]
    sectors = sources.shape[1]
    offset = lax.axis_index("sec") * owned
    labels = jnp.arange(sectors, dtype=jnp.int32)
    right_of = jnp.sum(
        jnp.where(sources[:, :, None] == labels[None, None, :], labels[None, :, None], 0), axis=1
    )
    own_sources = lax.dynamic_slice_in_dim(sources, offset, owned, 1)
    steps_total = lax.axis_size("site") // 4
    dim_all = sectors * width
    all_left, all_right, left_start, right_start = (
        lax.all_gather(canon_left, "sec", axis=1, tiled=True),
        lax.all_gather(canon_right, "sec", axis=1, tiled=True),
        lax.all_gather(left_seed[0], "sec", axis=0, tiled=True),
        lax.all_gather(right_seed[0], "sec", axis=0, tiled=True),
    )

    def chain_turn(count_now, state_tuple):
        left_hold, right_hold, left_last = state_tuple
        left_fresh = left_turn(left_hold, all_left, sources)
        right_fresh = right_turn(right_hold, all_right, right_of)
        left_moved = from_behind(left_fresh, "site", 1)
        right_moved = from_behind(right_fresh, "site", -1)
        return (left_moved, right_moved, left_fresh)

    env_cur, env_right, env_next = lax.fori_loop(
        0, steps_total, chain_turn, (left_start, right_start, left_start)
    )
    trace_cur = trace_sum(env_cur)
    trace_next = trace_sum(env_next)
    trace_right = trace_sum(env_right)
    next_own = lax.dynamic_slice_in_dim(env_next, offset, owned, 0)
    right_own = lax.dynamic_slice_in_dim(env_right, offset, owned, 0)
    cur_scaled = (env_cur.astype(jnp.float32) * (dim_all / trace_cur)).astype(jnp.bfloat16)
    next_scaled = (next_own.astype(jnp.float32) * (dim_all / trace_next)).astype(jnp.bfloat16)
    right_scaled = (right_own.astype(jnp.float32) * (dim_all / trace_right)).astype(jnp.bfloat16)
    chosen_left = jnp.take(cur_scaled, own_sources, axis=0)
    for repeat in range(NAPP):
        half_site = jnp.einsum(
            "skab,skbc->skac", chosen_left, site_now, preferred_element_type=jnp.float32
        ).astype(jnp.bfloat16)
        site_now = (
            jnp.einsum(
                "skab,kbc->skac", half_site, right_scaled, preferred_element_type=jnp.float32
            )
            + energy[:, None, None, None] * site_now.astype(jnp.float32)
        ).astype(jnp.bfloat16)
        half_bond = jnp.einsum(
            "kab,kbc->kac", next_scaled, bond_now, preferred_element_type=jnp.float32
        ).astype(jnp.bfloat16)
        bond_now = (
            jnp.einsum("kab,kbc->kac", half_bond, right_scaled, preferred_element_type=jnp.float32)
            + bond_add * bond_now.astype(jnp.float32)
        ).astype(jnp.bfloat16)
    gram_left = jnp.einsum("skab,skac->kbc", site_now, site_now, preferred_element_type=jnp.float32)
    gram_bond = jnp.einsum("kab,kac->kbc", bond_now, bond_now, preferred_element_type=jnp.float32)
    unit_left = jnp.matmul(
        bond_now.astype(jnp.float32), inverse_root(gram_bond), precision=lax.Precision.HIGHEST
    )
    factor_left = jnp.matmul(
        inverse_root(gram_left), jnp.swapaxes(unit_left, -1, -2), precision=lax.Precision.HIGHEST
    ).astype(jnp.bfloat16)
    left_new = jnp.einsum(
        "skab,kbc->skac", site_now, factor_left, preferred_element_type=jnp.float32
    ).astype(jnp.bfloat16)
    outer_terms = jnp.einsum(
        "skab,skcb->skac", site_now, site_now, preferred_element_type=jnp.float32
    )
    routing = (own_sources[:, :, None] == labels[None, None, :]).astype(jnp.float32)
    buffer_all = jnp.einsum("skm,skac->mac", routing, outer_terms, precision=lax.Precision.HIGHEST)
    previous = from_behind(bond_now, "site", 1)
    gram_part = sent_and_summed(buffer_all, "sec", 0)
    factor_part = right_polar(gram_part, previous)
    factor_right = collect(factor_part, "sec", 0)
    factor_chosen = jnp.take(factor_right, own_sources, axis=0)
    right_new = jnp.einsum(
        "skab,skbc->skac", factor_chosen, site_now, preferred_element_type=jnp.float32
    ).astype(jnp.bfloat16)
    return (left_new[None], right_new[None])


def solution(mesh):
    return jax.shard_map(
        per_device,
        mesh=mesh,
        in_specs=(
            P("site", None, "sec", None, None),
            P("site", None, "sec", None, None),
            P("site", None, "sec", None, None),
            P("site", "sec", None, None),
            P("site", "sec", None, None),
            P("site", "sec", None, None),
            P("site", None, None),
            P("site", None),
            P("site"),
        ),
        out_specs=(P("site", None, "sec", None, None), P("site", None, "sec", None, None)),
        check_vma=False,
    )
```

profile of v0, /device:TPU:2, one launch (start us, length us, event | category | flops | bytes accessed | tf_op | source)
XLA Modules:
  0.0 598.0 jit_solution(5434070529039616663)
XLA Ops:
  8.7 32.1 %all-gather = bf16[1,16,128,128]{3,2,0,1:T(8,128)(2,1)S(1)} all-gather(bf16[1,2,128,128]{3,2,0,1:T(8,128)(2,1)} %bitcast.417), channel_id=2, replica_groups=mesh['site'=32,'sec'=8] {'sec'}, dimensions={1}, use_global_device_ids=true | all-gather | bytes 589824 | tf_op jit(solution)/shard_map/all_gather | solution.py:130
  47.5 33.6 %all-gather.1 = bf16[1,16,128,128]{3,2,0,1:T(8,128)(2,1)S(1)} all-gather(bf16[1,2,128,128]{3,2,0,1:T(8,128)(2,1)S(1)} %bitcast.418), channel_id=3, replica_groups=mesh['site'=32,'sec'=8] {'sec'}, dimensions={1}, use_global_device_ids=true | all-gather | bytes 589824 | tf_op jit(solution)/shard_map/all_gather | solution.py:131
  91.3 44.1 %all-gather.7.cloned.1.call-done = bf16[1,4,16,128,128]{4,3,2,1,0:T(8,128)(2,1)} async-done(((bf16[1,4,2,128,128]{4,3,2,1,0:T(8,128)(2,1)}), bf16[1,4,16,128,128]{4,3,2,1,0:T(8,128)(2,1)}) %all-gather.7.cloned.1.call-update) | async-done | bytes 2097168 | tf_op jit(solution)/shard_map/all_gather | solution.py:128
  135.4 367.6 %while.16 = (s32[]{:T(128)}, bf16[16,128,128]{1,2,0:T(8,128)(2,1)S(1)}, bf16[16,128,128]{2,1,0:T(8,128)(2,1)S(1)}, bf16[16,128,128]{1,2,0:T(8,128)(2,1)}, s32[4,...) while((s32[]{:T(128)}, ...), condition=%wide.region_2.0_spmd, body=%wide.region_1.3_spmd.sunk | while | flops 1080042240 | bytes 51419656 | solution.py:142
  150.1 4.1 collective-permute-start.1
  166.7 3.1 convolution_add_fusion.13
  172.5 12.4 %collective-permute-done = bf16[16,128,128]{1,2,0:T(8,128)(2,1)S(1)} collective-permute-done((bf16[16,128,128]{1,2,0:T(8,128)(2,1)}, bf16[16,128,128]{1,2,0:T(8,128)(2,1)S(1)}, u32[]{:S(2)}, u32[]{:S(2)}) %collective-permute-start) | collective-permute-done | bytes 524320 | tf_op jit(solution)/shard_map/while/body/eval_jaxpr/ppermute | solution.py:13
  196.6 3.0 fusion.544
  212.2 3.1 convolution_add_fusion.13
  218.5 11.9 %collective-permute-done = bf16[16,128,128]{1,2,0:T(8,128)(2,1)S(1)} collective-permute-done((bf16[16,128,128]{1,2,0:T(8,128)(2,1)}, bf16[16,128,128]{1,2,0:T(8,128)(2,1)S(1)}, u32[]{:S(2)}, u32[]{:S(2)}) %collective-permute-start) | collective-permute-done | bytes 524320 | tf_op jit(solution)/shard_map/while/body/eval_jaxpr/ppermute | solution.py:13
  242.1 3.0 fusion.544
  257.6 3.1 convolution_add_fusion.13
  263.9 11.9 %collective-permute-done = bf16[16,128,128]{1,2,0:T(8,128)(2,1)S(1)} collective-permute-done((bf16[16,128,128]{1,2,0:T(8,128)(2,1)}, bf16[16,128,128]{1,2,0:T(8,128)(2,1)S(1)}, u32[]{:S(2)}, u32[]{:S(2)}) %collective-permute-start) | collective-permute-done | bytes 524320 | tf_op jit(solution)/shard_map/while/body/eval_jaxpr/ppermute | solution.py:13
  287.5 3.0 fusion.544
  303.0 3.1 convolution_add_fusion.13
  309.3 11.9 %collective-permute-done = bf16[16,128,128]{1,2,0:T(8,128)(2,1)S(1)} collective-permute-done((bf16[16,128,128]{1,2,0:T(8,128)(2,1)}, bf16[16,128,128]{1,2,0:T(8,128)(2,1)S(1)}, u32[]{:S(2)}, u32[]{:S(2)}) %collective-permute-start) | collective-permute-done | bytes 524320 | tf_op jit(solution)/shard_map/while/body/eval_jaxpr/ppermute | solution.py:13
  332.9 3.0 fusion.544
  348.5 3.1 convolution_add_fusion.13
  354.8 11.9 %collective-permute-done = bf16[16,128,128]{1,2,0:T(8,128)(2,1)S(1)} collective-permute-done((bf16[16,128,128]{1,2,0:T(8,128)(2,1)}, bf16[16,128,128]{1,2,0:T(8,128)(2,1)S(1)}, u32[]{:S(2)}, u32[]{:S(2)}) %collective-permute-start) | collective-permute-done | bytes 524320 | tf_op jit(solution)/shard_map/while/body/eval_jaxpr/ppermute | solution.py:13
  378.4 3.0 fusion.544
  393.9 3.1 convolution_add_fusion.13
  400.2 11.9 %collective-permute-done = bf16[16,128,128]{1,2,0:T(8,128)(2,1)S(1)} collective-permute-done((bf16[16,128,128]{1,2,0:T(8,128)(2,1)}, bf16[16,128,128]{1,2,0:T(8,128)(2,1)S(1)}, u32[]{:S(2)}, u32[]{:S(2)}) %collective-permute-start) | collective-permute-done | bytes 524320 | tf_op jit(solution)/shard_map/while/body/eval_jaxpr/ppermute | solution.py:13
  439.4 3.1 convolution_add_fusion.13
  445.7 11.9 %collective-permute-done = bf16[16,128,128]{1,2,0:T(8,128)(2,1)S(1)} collective-permute-done((bf16[16,128,128]{1,2,0:T(8,128)(2,1)}, bf16[16,128,128]{1,2,0:T(8,128)(2,1)S(1)}, u32[]{:S(2)}, u32[]{:S(2)}) %collective-permute-start) | collective-permute-done | bytes 524320 | tf_op jit(solution)/shard_map/while/body/eval_jaxpr/ppermute | solution.py:13
  484.8 3.1 convolution_add_fusion.13
  491.1 11.9 %collective-permute-done = bf16[16,128,128]{1,2,0:T(8,128)(2,1)S(1)} collective-permute-done((bf16[16,128,128]{1,2,0:T(8,128)(2,1)}, bf16[16,128,128]{1,2,0:T(8,128)(2,1)S(1)}, u32[]{:S(2)}, u32[]{:S(2)}) %collective-permute-start) | collective-permute-done | bytes 524320 | tf_op jit(solution)/shard_map/while/body/eval_jaxpr/ppermute | solution.py:13
  503.0 4.1 copy.176
  507.5 6.4 %copy.189 = f32[16,128,128]{0,2,1:T(8,128)} copy(bf16[16,128,128]{1,2,0:T(8,128)(2,1)S(1)} %copy-done.4) | data formatting | bytes 1572864 | tf_op jit(solution)/shard_map/convert_element_type | solution.py:58
  529.3 4.5 copy.180
  549.4 6.0 all-to-all-start
  577.1 4.7 all-to-all-start.1
  583.5 5.8 all-to-all-done.1
  (571 shorter events, 298.0 us)
Async XLA Ops:
  7.2 34.7 %copy-start.7 = (s32[1,4,16]{2,1,0:T(4,128)S(1)}, s32[1,4,16]{2,1,0:T(4,128)}, u32[]{:S(2)}) copy-start(s32[1,4,16]{2,1,0:T(4,128)} %param.21) | copy-start | bytes 772
  7.2 35.7 %copy-start.5 = (bf16[1,4,2,128,128]{4,3,2,1,0:T(8,128)(2,1)S(1)}, bf16[1,4,2,128,128]{4,3,2,1,0:T(8,128)(2,1)}, u32[]{:S(2)}) copy-start(bf16[1,4,2,128,128]{4,3,2,1,0:T(8,128)(2,1)} %param.17) | copy-start | bytes 786436
  7.2 40.3 %copy-start.10 = (bf16[1,2,128,128]{3,2,1,0:T(8,128)(2,1)S(1)}, bf16[1,2,128,128]{3,2,1,0:T(8,128)(2,1)}, u32[]{:S(2)}) copy-start(bf16[1,2,128,128]{3,2,1,0:T(8,128)(2,1)} %param.20) | copy-start | bytes 196612
  7.2 73.9 %all-gather.9.cloned.1.call-start = ((), (), s32[]{:S(2)}) async-start(), calls=%async_computation.3 | async-start | bytes 2359296 | tf_op jit(solution)/shard_map/all_gather | solution.py:129
  7.9 127.5 %all-gather.7.cloned.1.call-start = ((), (), s32[]{:S(2)}) async-start(), calls=%async_computation.2 | async-start | bytes 2359296 | tf_op jit(solution)/shard_map/all_gather | solution.py:128
  150.1 22.4 %collective-permute-start.1 = (bf16[16,128,128]{2,1,0:T(8,128)(2,1)}, bf16[16,128,128]{2,1,0:T(8,128)(2,1)S(1)}, u32[]{:S(2)}, u32[]{:S(2)}) collective-permute-start(bf16[16,128,128]{2,1,0:T(8,128)(2,1)} %fusion.544), channel_id=1, source_target_pairs={{8,0},{16,8},{24,16},{32,24},{40,32},{48,40},{56,48},{64,56},{72,6... | collective-permute-start | bytes 1572872 | tf_op jit(solution)/shard_map/while/body/eval_jaxpr/ppermute | solution.py:13
  169.8 15.2 %copy-start.9 = (s32[4,16]{1,0:T(4,128)S(1)}, s32[4,16]{1,0:T(4,128)}, u32[]{:S(2)}) copy-start(s32[4,16]{1,0:T(4,128)} %copy-done.8) | copy-start | bytes 772 | tf_op jit(solution)/shard_map/while
  172.5 12.4 %collective-permute-start = (bf16[16,128,128]{1,2,0:T(8,128)(2,1)}, bf16[16,128,128]{1,2,0:T(8,128)(2,1)S(1)}, u32[]{:S(2)}, u32[]{:S(2)}) collective-permute-start(bf16[16,128,128]{1,2,0:T(8,128)(2,1)} %fusion.542), channel_id=1, source_target_pairs={{248,0},{0,8},{8,16},{16,24},{24,32},{32,40},{40,48},{48,56},{56,6... | collective-permute-start | bytes 1572872 | tf_op jit(solution)/shard_map/while/body/eval_jaxpr/ppermute | solution.py:13
  199.7 18.8 %collective-permute-start.1 = (bf16[16,128,128]{2,1,0:T(8,128)(2,1)}, bf16[16,128,128]{2,1,0:T(8,128)(2,1)S(1)}, u32[]{:S(2)}, u32[]{:S(2)}) collective-permute-start(bf16[16,128,128]{2,1,0:T(8,128)(2,1)} %fusion.544), channel_id=1, source_target_pairs={{8,0},{16,8},{24,16},{32,24},{40,32},{48,40},{56,48},{64,56},{72,6... | collective-permute-start | bytes 1572872 | tf_op jit(solution)/shard_map/while/body/eval_jaxpr/ppermute | solution.py:13
  215.2 15.2 %copy-start.9 = (s32[4,16]{1,0:T(4,128)S(1)}, s32[4,16]{1,0:T(4,128)}, u32[]{:S(2)}) copy-start(s32[4,16]{1,0:T(4,128)} %copy-done.8) | copy-start | bytes 772 | tf_op jit(solution)/shard_map/while
  217.9 12.4 %collective-permute-start = (bf16[16,128,128]{1,2,0:T(8,128)(2,1)}, bf16[16,128,128]{1,2,0:T(8,128)(2,1)S(1)}, u32[]{:S(2)}, u32[]{:S(2)}) collective-permute-start(bf16[16,128,128]{1,2,0:T(8,128)(2,1)} %fusion.542), channel_id=1, source_target_pairs={{248,0},{0,8},{8,16},{16,24},{24,32},{32,40},{40,48},{48,56},{56,6... | collective-permute-start | bytes 1572872 | tf_op jit(solution)/shard_map/while/body/eval_jaxpr/ppermute | solution.py:13
  245.1 18.8 %collective-permute-start.1 = (bf16[16,128,128]{2,1,0:T(8,128)(2,1)}, bf16[16,128,128]{2,1,0:T(8,128)(2,1)S(1)}, u32[]{:S(2)}, u32[]{:S(2)}) collective-permute-start(bf16[16,128,128]{2,1,0:T(8,128)(2,1)} %fusion.544), channel_id=1, source_target_pairs={{8,0},{16,8},{24,16},{32,24},{40,32},{48,40},{56,48},{64,56},{72,6... | collective-permute-start | bytes 1572872 | tf_op jit(solution)/shard_map/while/body/eval_jaxpr/ppermute | solution.py:13
  260.7 15.2 %copy-start.9 = (s32[4,16]{1,0:T(4,128)S(1)}, s32[4,16]{1,0:T(4,128)}, u32[]{:S(2)}) copy-start(s32[4,16]{1,0:T(4,128)} %copy-done.8) | copy-start | bytes 772 | tf_op jit(solution)/shard_map/while
  263.4 12.4 %collective-permute-start = (bf16[16,128,128]{1,2,0:T(8,128)(2,1)}, bf16[16,128,128]{1,2,0:T(8,128)(2,1)S(1)}, u32[]{:S(2)}, u32[]{:S(2)}) collective-permute-start(bf16[16,128,128]{1,2,0:T(8,128)(2,1)} %fusion.542), channel_id=1, source_target_pairs={{248,0},{0,8},{8,16},{16,24},{24,32},{32,40},{40,48},{48,56},{56,6... | collective-permute-start | bytes 1572872 | tf_op jit(solution)/shard_map/while/body/eval_jaxpr/ppermute | solution.py:13
  290.5 18.8 %collective-permute-start.1 = (bf16[16,128,128]{2,1,0:T(8,128)(2,1)}, bf16[16,128,128]{2,1,0:T(8,128)(2,1)S(1)}, u32[]{:S(2)}, u32[]{:S(2)}) collective-permute-start(bf16[16,128,128]{2,1,0:T(8,128)(2,1)} %fusion.544), channel_id=1, source_target_pairs={{8,0},{16,8},{24,16},{32,24},{40,32},{48,40},{56,48},{64,56},{72,6... | collective-permute-start | bytes 1572872 | tf_op jit(solution)/shard_map/while/body/eval_jaxpr/ppermute | solution.py:13
  306.1 15.2 %copy-start.9 = (s32[4,16]{1,0:T(4,128)S(1)}, s32[4,16]{1,0:T(4,128)}, u32[]{:S(2)}) copy-start(s32[4,16]{1,0:T(4,128)} %copy-done.8) | copy-start | bytes 772 | tf_op jit(solution)/shard_map/while
  308.8 12.4 %collective-permute-start = (bf16[16,128,128]{1,2,0:T(8,128)(2,1)}, bf16[16,128,128]{1,2,0:T(8,128)(2,1)S(1)}, u32[]{:S(2)}, u32[]{:S(2)}) collective-permute-start(bf16[16,128,128]{1,2,0:T(8,128)(2,1)} %fusion.542), channel_id=1, source_target_pairs={{248,0},{0,8},{8,16},{16,24},{24,32},{32,40},{40,48},{48,56},{56,6... | collective-permute-start | bytes 1572872 | tf_op jit(solution)/shard_map/while/body/eval_jaxpr/ppermute | solution.py:13
  336.0 18.8 %collective-permute-start.1 = (bf16[16,128,128]{2,1,0:T(8,128)(2,1)}, bf16[16,128,128]{2,1,0:T(8,128)(2,1)S(1)}, u32[]{:S(2)}, u32[]{:S(2)}) collective-permute-start(bf16[16,128,128]{2,1,0:T(8,128)(2,1)} %fusion.544), channel_id=1, source_target_pairs={{8,0},{16,8},{24,16},{32,24},{40,32},{48,40},{56,48},{64,56},{72,6... | collective-permute-start | bytes 1572872 | tf_op jit(solution)/shard_map/while/body/eval_jaxpr/ppermute | solution.py:13
  351.5 15.2 %copy-start.9 = (s32[4,16]{1,0:T(4,128)S(1)}, s32[4,16]{1,0:T(4,128)}, u32[]{:S(2)}) copy-start(s32[4,16]{1,0:T(4,128)} %copy-done.8) | copy-start | bytes 772 | tf_op jit(solution)/shard_map/while
  354.3 12.4 %collective-permute-start = (bf16[16,128,128]{1,2,0:T(8,128)(2,1)}, bf16[16,128,128]{1,2,0:T(8,128)(2,1)S(1)}, u32[]{:S(2)}, u32[]{:S(2)}) collective-permute-start(bf16[16,128,128]{1,2,0:T(8,128)(2,1)} %fusion.542), channel_id=1, source_target_pairs={{248,0},{0,8},{8,16},{16,24},{24,32},{32,40},{40,48},{48,56},{56,6... | collective-permute-start | bytes 1572872 | tf_op jit(solution)/shard_map/while/body/eval_jaxpr/ppermute | solution.py:13
  381.4 18.8 %collective-permute-start.1 = (bf16[16,128,128]{2,1,0:T(8,128)(2,1)}, bf16[16,128,128]{2,1,0:T(8,128)(2,1)S(1)}, u32[]{:S(2)}, u32[]{:S(2)}) collective-permute-start(bf16[16,128,128]{2,1,0:T(8,128)(2,1)} %fusion.544), channel_id=1, source_target_pairs={{8,0},{16,8},{24,16},{32,24},{40,32},{48,40},{56,48},{64,56},{72,6... | collective-permute-start | bytes 1572872 | tf_op jit(solution)/shard_map/while/body/eval_jaxpr/ppermute | solution.py:13
  397.0 15.2 %copy-start.9 = (s32[4,16]{1,0:T(4,128)S(1)}, s32[4,16]{1,0:T(4,128)}, u32[]{:S(2)}) copy-start(s32[4,16]{1,0:T(4,128)} %copy-done.8) | copy-start | bytes 772 | tf_op jit(solution)/shard_map/while
  399.7 12.4 %collective-permute-start = (bf16[16,128,128]{1,2,0:T(8,128)(2,1)}, bf16[16,128,128]{1,2,0:T(8,128)(2,1)S(1)}, u32[]{:S(2)}, u32[]{:S(2)}) collective-permute-start(bf16[16,128,128]{1,2,0:T(8,128)(2,1)} %fusion.542), channel_id=1, source_target_pairs={{248,0},{0,8},{8,16},{16,24},{24,32},{32,40},{40,48},{48,56},{56,6... | collective-permute-start | bytes 1572872 | tf_op jit(solution)/shard_map/while/body/eval_jaxpr/ppermute | solution.py:13
  426.9 18.8 %collective-permute-start.1 = (bf16[16,128,128]{2,1,0:T(8,128)(2,1)}, bf16[16,128,128]{2,1,0:T(8,128)(2,1)S(1)}, u32[]{:S(2)}, u32[]{:S(2)}) collective-permute-start(bf16[16,128,128]{2,1,0:T(8,128)(2,1)} %fusion.544), channel_id=1, source_target_pairs={{8,0},{16,8},{24,16},{32,24},{40,32},{48,40},{56,48},{64,56},{72,6... | collective-permute-start | bytes 1572872 | tf_op jit(solution)/shard_map/while/body/eval_jaxpr/ppermute | solution.py:13
  442.4 15.2 %copy-start.9 = (s32[4,16]{1,0:T(4,128)S(1)}, s32[4,16]{1,0:T(4,128)}, u32[]{:S(2)}) copy-start(s32[4,16]{1,0:T(4,128)} %copy-done.8) | copy-start | bytes 772 | tf_op jit(solution)/shard_map/while
  445.1 12.4 %collective-permute-start = (bf16[16,128,128]{1,2,0:T(8,128)(2,1)}, bf16[16,128,128]{1,2,0:T(8,128)(2,1)S(1)}, u32[]{:S(2)}, u32[]{:S(2)}) collective-permute-start(bf16[16,128,128]{1,2,0:T(8,128)(2,1)} %fusion.542), channel_id=1, source_target_pairs={{248,0},{0,8},{8,16},{16,24},{24,32},{32,40},{40,48},{48,56},{56,6... | collective-permute-start | bytes 1572872 | tf_op jit(solution)/shard_map/while/body/eval_jaxpr/ppermute | solution.py:13
  472.3 18.8 %collective-permute-start.1 = (bf16[16,128,128]{2,1,0:T(8,128)(2,1)}, bf16[16,128,128]{2,1,0:T(8,128)(2,1)S(1)}, u32[]{:S(2)}, u32[]{:S(2)}) collective-permute-start(bf16[16,128,128]{2,1,0:T(8,128)(2,1)} %fusion.544), channel_id=1, source_target_pairs={{8,0},{16,8},{24,16},{32,24},{40,32},{48,40},{56,48},{64,56},{72,6... | collective-permute-start | bytes 1572872 | tf_op jit(solution)/shard_map/while/body/eval_jaxpr/ppermute | solution.py:13
  487.9 15.2 %copy-start.9 = (s32[4,16]{1,0:T(4,128)S(1)}, s32[4,16]{1,0:T(4,128)}, u32[]{:S(2)}) copy-start(s32[4,16]{1,0:T(4,128)} %copy-done.8) | copy-start | bytes 772 | tf_op jit(solution)/shard_map/while
  490.6 12.4 %collective-permute-start = (bf16[16,128,128]{1,2,0:T(8,128)(2,1)}, bf16[16,128,128]{1,2,0:T(8,128)(2,1)S(1)}, u32[]{:S(2)}, u32[]{:S(2)}) collective-permute-start(bf16[16,128,128]{1,2,0:T(8,128)(2,1)} %fusion.542), channel_id=1, source_target_pairs={{248,0},{0,8},{8,16},{16,24},{24,32},{32,40},{40,48},{48,56},{56,6... | collective-permute-start | bytes 1572872 | tf_op jit(solution)/shard_map/while/body/eval_jaxpr/ppermute | solution.py:13
  520.8 35.7 %collective-permute-start.2 = (bf16[2,128,128]{2,1,0:T(8,128)(2,1)S(1)}, bf16[2,128,128]{2,1,0:T(8,128)(2,1)S(1)}, u32[]{:S(2)}, u32[]{:S(2)}) collective-permute-start(bf16[2,128,128]{2,1,0:T(8,128)(2,1)S(1)} %fusion.132), channel_id=1, source_target_pairs={{248,0},{0,8},{8,16},{16,24},{24,32},{32,40},{40,48},{48,56},{56,6... | collective-permute-start | bytes 196616 | tf_op jit(solution)/shard_map/ppermute | solution.py:13
  549.4 17.7 %all-to-all-start = ((f32[8,2,128,128]{3,1,2,0:T(2,128)}), f32[8,2,128,128]{3,1,2,0:T(2,128)S(1)}, u32[]{:S(2)}, u32[]{:S(2)}) async-start(f32[8,2,128,128]{3,1,2,0:T(2,128)} %copy.199), calls=%async_computation | async-start | bytes 2097152 | tf_op jit(solution)/shard_map/all_to_all | solution.py:24
  577.1 12.2 %all-to-all-start.1 = ((bf16[8,2,128,128]{3,2,1,0:T(8,128)(2,1)}), bf16[8,2,128,128]{3,2,1,0:T(8,128)(2,1)S(1)}, u32[]{:S(2)}, u32[]{:S(2)}) async-start(bf16[8,2,128,128]{3,2,1,0:T(8,128)(2,1)} %broadcast_in_dim.64), calls=%async_computation.1 | async-start | bytes 1048576 | tf_op jit(solution)/shard_map/all_to_all | solution.py:36
  (88 other events, 328.3 us)
Sparse Core Ops, SparseCore 0:
  9.8 69.5 all-gather.8
  81.1 54.2 all-gather.6
where the time goes:
time: 609 us; the launch traced here: 598 us
  matrix products  207 us (34%)
  waiting for transfers between devices  149 us (24%)
  local copies, waits for them, and re-layouts  114 us (19%)
  blocking collectives  65.6 us (11%)
  other arithmetic  24.3 us (4%)
  starting transfers between devices  18.7 us (3%)
  between operations  18.1 us (3%)
    ppermute x17, waiting for transfers between devices, from_behind(): return lax.ppermute(block, axis, route)  95.9 us
    dot_general x32, matrix products, left_turn(): jnp.einsum('kba,kbc->kac', tensor_blocks[physical], product, preferred_el...  90.6 us
    dot_general x32, matrix products, right_turn(): jnp.einsum('kac,kdc->kad', product, picked, preferred_element_type=jnp.fl...  79 us
    gather x32, local copies, waits for them, and re-layouts, left_turn(): chosen = jnp.take(hold_full, indices[physical], axis=0)  45.2 us
    all_gather x1, waiting for transfers between devices, per_device(): lax.all_gather(canon_left, 'sec', axis=1, tiled=True)  44.1 us
    all_gather x1, blocking collectives, per_device(): lax.all_gather(right_seed[0], 'sec', axis=0, tiled=True)  33.6 us
    gather x32, local copies, waits for them, and re-layouts, right_turn(): env_chosen = jnp.take(hold_full, indices[physical], axis=0)  33 us
    all_gather x1, blocking collectives, per_device(): lax.all_gather(left_seed[0], 'sec', axis=0, tiled=True)  32.1 us
  transfers between devices with their start and end apart: 21, of which 11 were waited for; matrix products, arithmetic and copies ran while one was open for 33% of the time, Pallas kernels for 0%

commit v1 on v0

--- a/solution.py
+++ b/solution.py
@@ -1,10 +1,16 @@
+import functools
+
 import jax
 import jax.numpy as jnp
 from jax import lax
+from jax.experimental import pallas as pl
+from jax.experimental.pallas import tpu as pltpu
 from jax.sharding import PartitionSpec as P
 
 NSI = 10
 NAPP = 2
+CHUNKS = 4
+MESH = pl.DeviceIdType.MESH
 
 
 def from_behind(block, axis, distance):
@@ -54,45 +60,223 @@
     return lower_part / jnp.sqrt(scaling)
 
 
-def trace_sum(blocks):
-    return jnp.sum(jnp.diagonal(blocks.astype(jnp.float32), axis1=1, axis2=2))
-
-
-def left_turn(hold_full, tensor_blocks, indices):
-    running = jnp.zeros(tensor_blocks.shape[1:], jnp.float32)
-    for physical in range(tensor_blocks.shape[0]):
-        chosen = jnp.take(hold_full, indices[physical], axis=0)
-        product = jnp.einsum(
-            "kab,kbc->kac", chosen, tensor_blocks[physical], preferred_element_type=jnp.float32
-        ).astype(jnp.bfloat16)
-        running = running + jnp.einsum(
-            "kba,kbc->kac", tensor_blocks[physical], product, preferred_element_type=jnp.float32
-        )
-    return running.astype(jnp.bfloat16)
-
-
-def right_turn(hold_full, tensor_all, indices):
-    running = jnp.zeros((indices.shape[1],) + hold_full.shape[1:], jnp.float32)
-    for physical in range(tensor_all.shape[0]):
-        picked = jnp.take(tensor_all[physical], indices[physical], axis=0)
-        env_chosen = jnp.take(hold_full, indices[physical], axis=0)
-        product = jnp.einsum(
-            "kab,kbc->kac", picked, env_chosen, preferred_element_type=jnp.float32
-        ).astype(jnp.bfloat16)
-        running = running + jnp.einsum(
-            "kac,kdc->kad", product, picked, preferred_element_type=jnp.float32
-        )
-    return running.astype(jnp.bfloat16)
-
-
-def right_polar(gram_right, previous):
-    gram_prev = jnp.einsum("kab,kcb->kac", previous, previous, preferred_element_type=jnp.float32)
-    unit_right = jnp.matmul(
-        inverse_root(gram_prev), previous.astype(jnp.float32), precision=lax.Precision.HIGHEST
-    )
-    return jnp.matmul(
-        jnp.swapaxes(unit_right, -1, -2), inverse_root(gram_right), precision=lax.Precision.HIGHEST
-    ).astype(jnp.bfloat16)
+def env_kernel(
+    sites, secs, steps,
+    tab, canon_l, canon_r, seed_l, seed_r,
+    cur_out, nxt_out, rgt_out,
+    own_c, own_s, tall, wab, hold, fresh, pbuf, give, got_n, got_r,
+    loc_sem, gsend, grecv, ssend, srecv, tsend, trecv, xsend, xrecv,
+):
+    site, sec = lax.axis_index("site"), lax.axis_index("sec")
+    role = lax.rem(sec, 2)
+    row = sec // 2
+    rows = secs // 2
+    phys, owned, width = canon_l.shape[0], canon_l.shape[1], canon_l.shape[2]
+    sectors = secs * owned
+    per = sectors // CHUNKS
+    target = lax.rem(site + 1 - 2 * role + sites, sites)
+    source = lax.rem(site - 1 + 2 * role + sites, sites)
+    peer_sec = row * 2 + 1 - role
+
+    loads = [
+        pltpu.make_async_copy(canon_l, own_c.at[0], loc_sem.at[0]),
+        pltpu.make_async_copy(canon_r, own_c.at[1], loc_sem.at[1]),
+    ]
+    for load in loads:
+        load.start()
+    for i in range(owned):
+        own_s[0, i] = seed_l[i]
+        own_s[1, i] = seed_r[i].T
+
+    barrier = pltpu.get_barrier_semaphore()
+    others = [(dy, e) for dy in range(rows) for e in range(2) if (dy, e) != (0, 0)]
+
+    def sec_of(dy, e):
+        other_role = role + e - 2 * role * e
+        return lax.rem(row + dy, rows) * 2 + other_role, other_role
+
+    for dy, e in others:
+        pl.semaphore_signal(barrier, inc=1, device_id=(site, sec_of(dy, e)[0]), device_id_type=MESH)
+    for other in (target, source):
+        pl.semaphore_signal(barrier, inc=1, device_id=(other, sec), device_id_type=MESH)
+    pl.semaphore_wait(barrier, len(others) + 2)
+
+    place = pl.ds(sec * owned, owned)
+    sent = []
+    for n, (dy, e) in enumerate(others):
+        to, to_role = sec_of(dy, e)
+        sent.append(pltpu.make_async_remote_copy(
+            src_ref=own_s.at[to_role], dst_ref=hold.at[0, place],
+            send_sem=ssend.at[n], recv_sem=srecv.at[n],
+            device_id=(site, to), device_id_type=MESH))
+        sent[-1].start()
+    for load in loads:
+        load.wait()
+    keep = [
+        pltpu.make_async_copy(own_c.at[role], tall.at[:, place], loc_sem.at[0]),
+        pltpu.make_async_copy(own_s.at[role], hold.at[0, place], loc_sem.at[1]),
+    ]
+    for n, (dy, e) in enumerate(others):
+        to, to_role = sec_of(dy, e)
+        sent.append(pltpu.make_async_remote_copy(
+            src_ref=own_c.at[to_role], dst_ref=tall.at[:, place],
+            send_sem=gsend.at[n], recv_sem=grecv.at[n],
+            device_id=(site, to), device_id_type=MESH))
+        sent[-1].start()
+    for copy in keep:
+        copy.start()
+    for copy in keep:
+        copy.wait()
+    for copy in sent:
+        copy.wait_recv()
+
+    def arrange(i, carry):
+        for s in range(phys):
+            cols = slice(s * width, (s + 1) * width)
+            wab[role, i, :, cols] = tall[s, tab[1, s, i]]
+            wab[1 - role, i, :, cols] = tall[s, i].T
+        return carry
+
+    lax.fori_loop(0, sectors, arrange, 0)
+
+    def chunk_copy(t, c):
+        part = pl.ds(c * per, per)
+        return pltpu.make_async_remote_copy(
+            src_ref=fresh.at[t, part], dst_ref=hold.at[t + 1, part],
+            send_sem=tsend.at[t, c], recv_sem=trecv.at[t, c],
+            device_id=(target, sec), device_id_type=MESH)
+
+    def turn(t, carry):
+        for c in range(CHUNKS):
+            @pl.when(t > 0)
+            def _():
+                chunk_copy(t - 1, c).wait_recv()
+
+            for i in range(c * per, (c + 1) * per):
+                product = jnp.dot(
+                    hold[t, i], wab[0, i], preferred_element_type=jnp.float32
+                ).astype(jnp.bfloat16)
+                for s in range(phys):
+                    pbuf[i, s] = product[:, s * width : (s + 1) * width]
+        for c in range(CHUNKS):
+            for o in range(c * per, (c + 1) * per):
+                stack = jnp.concatenate([pbuf[tab[role, s, o], s] for s in range(phys)], axis=0)
+                fresh[t, o] = jnp.dot(
+                    wab[1, o], stack, preferred_element_type=jnp.float32
+                ).astype(jnp.bfloat16)
+            chunk_copy(t, c).start()
+        return carry
+
+    lax.fori_loop(0, steps, turn, 0)
+    for c in range(CHUNKS):
+        chunk_copy(steps - 1, c).wait_recv()
+
+    rows_at = lax.broadcasted_iota(jnp.int32, (width, width), 0)
+    cols_at = lax.broadcasted_iota(jnp.int32, (width, width), 1)
+    diagonal = rows_at == cols_at
+
+    def factor(ref, t):
+        total = ref[t, 0].astype(jnp.float32)
+        for i in range(1, sectors):
+            total = total + ref[t, i].astype(jnp.float32)
+        return (sectors * width) / jnp.sum(jnp.where(diagonal, total, 0.0))
+
+    own_at = sec * owned
+    peer_at = peer_sec * owned
+    cur_copies = [pltpu.make_async_remote_copy(
+        src_ref=give.at[pl.ds(c * per, per)], dst_ref=cur_out.at[pl.ds(c * per, per)],
+        send_sem=xsend.at[c], recv_sem=xrecv.at[c],
+        device_id=(site, peer_sec), device_id_type=MESH) for c in range(CHUNKS)]
+    nxt_copy = pltpu.make_async_remote_copy(
+        src_ref=got_r, dst_ref=got_n,
+        send_sem=xsend.at[CHUNKS], recv_sem=xrecv.at[CHUNKS],
+        device_id=(site, peer_sec), device_id_type=MESH)
+
+    @pl.when(role == 0)
+    def _():
+        scale_next = factor(fresh, steps - 1)
+        for i in range(owned):
+            got_r[i] = (fresh[steps - 1, peer_at + i].astype(jnp.float32) * scale_next).astype(jnp.bfloat16)
+            nxt_out[i] = (fresh[steps - 1, own_at + i].astype(jnp.float32) * scale_next).astype(jnp.bfloat16)
+        nxt_copy.start()
+        scale_cur = factor(hold, steps)
+        for c in range(CHUNKS):
+            for i in range(c * per, (c + 1) * per):
+                give[i] = (hold[steps, i].astype(jnp.float32) * scale_cur).astype(jnp.bfloat16)
+            cur_copies[c].start()
+        for i in range(sectors):
+            cur_out[i] = give[i]
+        nxt_copy.wait_recv()
+        for i in range(owned):
+            rgt_out[i] = got_n[i].T
+        nxt_copy.wait_send()
+        for copy in cur_copies:
+            copy.wait_send()
+
+    @pl.when(role == 1)
+    def _():
+        scale_right = factor(hold, steps)
+        for i in range(owned):
+            got_r[i] = (hold[steps, peer_at + i].astype(jnp.float32) * scale_right).astype(jnp.bfloat16)
+        nxt_copy.start()
+        for i in range(owned):
+            rgt_out[i] = (hold[steps, own_at + i].astype(jnp.float32) * scale_right).astype(jnp.bfloat16).T
+        nxt_copy.wait_recv()
+        for i in range(owned):
+            nxt_out[i] = got_n[i]
+        nxt_copy.wait_send()
+        for copy in cur_copies:
+            copy.wait_recv()
+
+    for copy in sent:
+        copy.wait_send()
+
+    def drain(t, carry):
+        for c in range(CHUNKS):
+            chunk_copy(t, c).wait_send()
+        return carry
+
+    lax.fori_loop(0, steps, drain, 0)
+
+
+def environments(canon_l, canon_r, seed_l, seed_r, tables):
+    sites, secs = lax.axis_size("site"), lax.axis_size("sec")
+    steps = sites // 4
+    phys, owned, width = canon_l.shape[:3]
+    sectors = owned * secs
+    bf16 = jnp.bfloat16
+    block = (width, width)
+    dma = pltpu.SemaphoreType.DMA
+    vmem = pl.BlockSpec(memory_space=pltpu.VMEM)
+    hbm = pl.BlockSpec(memory_space=pl.ANY)
+    return pl.pallas_call(
+        functools.partial(env_kernel, sites, secs, steps),
+        out_shape=(
+            jax.ShapeDtypeStruct((sectors, *block), bf16),
+            jax.ShapeDtypeStruct((owned, *block), bf16),
+            jax.ShapeDtypeStruct((owned, *block), bf16),
+        ),
+        in_specs=[pl.BlockSpec(memory_space=pltpu.SMEM), hbm, hbm, vmem, vmem],
+        out_specs=(vmem, vmem, vmem),
+        scratch_shapes=[
+            pltpu.VMEM((2, phys, owned, *block), bf16),
+            pltpu.VMEM((2, owned, *block), bf16),
+            pltpu.VMEM((phys, sectors, *block), bf16),
+            pltpu.VMEM((2, sectors, width, phys * width), bf16),
+            pltpu.VMEM((steps + 1, sectors, *block), bf16),
+            pltpu.VMEM((steps, sectors, *block), bf16),
+            pltpu.VMEM((sectors, phys, *block), bf16),
+            pltpu.VMEM((sectors, *block), bf16),
+            pltpu.VMEM((owned, *block), bf16),
+            pltpu.VMEM((owned, *block), bf16),
+            dma((2,)), dma((secs - 1,)), dma((secs - 1,)), dma((secs - 1,)), dma((secs - 1,)),
+            dma((steps, CHUNKS)), dma((steps, CHUNKS)), dma((CHUNKS + 1,)), dma((CHUNKS + 1,)),
+        ],
+        compiler_params=pltpu.CompilerParams(
+            collective_id=0, has_side_effects=True, vmem_limit_bytes=48 * 1024 * 1024
+        ),
+        name="environments",
+    )(tables, canon_l, canon_r, seed_l, seed_r)
 
 
 def per_device(
@@ -114,7 +298,6 @@
     energy = onsite[0]
     bond_add = bond_shift[0]
     owned = canon_left.shape[1]
-    width = canon_left.shape[2]
     sectors = sources.shape[1]
     offset = lax.axis_index("sec") * owned
     labels = jnp.arange(sectors, dtype=jnp.int32)
@@ -122,34 +305,9 @@
         jnp.where(sources[:, :, None] == labels[None, None, :], labels[None, :, None], 0), axis=1
     )
     own_sources = lax.dynamic_slice_in_dim(sources, offset, owned, 1)
-    steps_total = lax.axis_size("site") // 4
-    dim_all = sectors * width
-    all_left, all_right, left_start, right_start = (
-        lax.all_gather(canon_left, "sec", axis=1, tiled=True),
-        lax.all_gather(canon_right, "sec", axis=1, tiled=True),
-        lax.all_gather(left_seed[0], "sec", axis=0, tiled=True),
-        lax.all_gather(right_seed[0], "sec", axis=0, tiled=True),
-    )
-
-    def chain_turn(count_now, state_tuple):
-        left_hold, right_hold, left_last = state_tuple
-        left_fresh = left_turn(left_hold, all_left, sources)
-        right_fresh = right_turn(right_hold, all_right, right_of)
-        left_moved = from_behind(left_fresh, "site", 1)
-        right_moved = from_behind(right_fresh, "site", -1)
-        return (left_moved, right_moved, left_fresh)
-
-    env_cur, env_right, env_next = lax.fori_loop(
-        0, steps_total, chain_turn, (left_start, right_start, left_start)
-    )
-    trace_cur = trace_sum(env_cur)
-    trace_next = trace_sum(env_next)
-    trace_right = trace_sum(env_right)
-    next_own = lax.dynamic_slice_in_dim(env_next, offset, owned, 0)
-    right_own = lax.dynamic_slice_in_dim(env_right, offset, owned, 0)
-    cur_scaled = (env_cur.astype(jnp.float32) * (dim_all / trace_cur)).astype(jnp.bfloat16)
-    next_scaled = (next_own.astype(jnp.float32) * (dim_all / trace_next)).astype(jnp.bfloat16)
-    right_scaled = (right_own.astype(jnp.float32) * (dim_all / trace_right)).astype(jnp.bfloat16)
+    cur_scaled, next_scaled, right_scaled = environments(
+        canon_left, canon_right, left_seed[0], right_seed[0], jnp.stack([sources, right_of])
+    )
     chosen_left = jnp.take(cur_scaled, own_sources, axis=0)
     for repeat in range(NAPP):
         half_site = jnp.einsum(
@@ -184,9 +342,11 @@
     )
     routing = (own_sources[:, :, None] == labels[None, None, :]).astype(jnp.float32)
     buffer_all = jnp.einsum("skm,skac->mac", routing, outer_terms, precision=lax.Precision.HIGHEST)
-    previous = from_behind(bond_now, "site", 1)
-    gram_part = sent_and_summed(buffer_all, "sec", 0)
-    factor_part = right_polar(gram_part, previous)
+    unit_right = from_behind(unit_left, "site", 1)
+    gram_right = sent_and_summed(buffer_all, "sec", 0)
+    factor_part = jnp.matmul(
+        jnp.swapaxes(unit_right, -1, -2), inverse_root(gram_right), precision=lax.Precision.HIGHEST
+    ).astype(jnp.bfloat16)
     factor_right = collect(factor_part, "sec", 0)
     factor_chosen = jnp.take(factor_right, own_sources, axis=0)
     right_new = jnp.einsum(

time: 609 us -> 165 us (0.27); the launches traced: 598 us -> 164 us
  matrix products: 207 us -> 29.4 us
  waiting for transfers between devices: 149 us -> 8.04 us
  local copies, waits for them, and re-layouts: 114 us -> 9.13 us
  Pallas kernels: 0 us -> 103 us
  blocking collectives: 65.6 us -> 0 us
  other arithmetic: 24.3 us -> 0.82 us
  between operations: 18.1 us -> 2.21 us
  starting transfers between devices: 18.7 us -> 11.1 us
    dot_general x67 -> x1, matrix products: 170 us -> 0.39 us  [per_device(): jnp.matmul(jnp.swapaxes(unit_right, -1, -2), inverse_root(gram_right), pr...]
    pallas_call x0 -> x1, Pallas kernels: none -> 103 us  [environments(): pl.pallas_call(functools.partial(env_kernel, sites, secs, steps), out_sha...]
    ppermute x17 -> x1, waiting for transfers between devices: 95.9 us -> 0.01 us  [from_behind(): return lax.ppermute(block, axis, route)]
    gather x71 -> x0, local copies, waits for them, and re-layouts: 87.5 us -> none  [the longest x32 45.2 us: left_turn(): chosen = jnp.take(hold_full, indices[physical], axis=0)]
    all_gather x2 -> x0, blocking collectives: 65.6 us -> none  [the longest x1 33.6 us: per_device(): lax.all_gather(right_seed[0], 'sec', axis=0, tiled=True)]
    all_gather x2 -> x0, waiting for transfers between devices: 44.1 us -> none  [the longest x1 44.1 us: per_device(): lax.all_gather(canon_left, 'sec', axis=1, tiled=True)]
    convert_element_type x3 -> x0, local copies, waits for them, and re-layouts: 15 us -> none  [the longest x2 10.5 us: trace_sum(): return jnp.sum(jnp.diagonal(blocks.astype(jnp.float32), axis1=1, axis2=2))]
    and x17 -> x0, other arithmetic: 10.2 us -> none  [the longest x8 4.83 us: left_turn(): chosen = jnp.take(hold_full, indices[physical], axis=0)]
  transfers between devices with their start and end apart: 21 -> 3, of which waited for: 11 -> 1; matrix products, arithmetic and copies ran while one was open for 33% -> 17% of each run, Pallas kernels for 0% -> 0%
where the time goes in v1:
time: 165 us; the launch traced here: 164 us
  Pallas kernels  103 us (62%)
  matrix products  29.4 us (18%)
  starting transfers between devices  11.1 us (7%)
  local copies, waits for them, and re-layouts  9.13 us (6%)
  waiting for transfers between devices  8.04 us (5%)
  between operations  2.21 us (1%)
    pallas_call x1, Pallas kernels, environments(): pl.pallas_call(functools.partial(env_kernel, sites, secs, steps), out_sha...  103 us
    dot_general x30, matrix products, inverse_root(): jnp.matmul(lower_part, upper_part, precision=lax.Precision.HIGHEST)  8.28 us
    all_to_all x1, waiting for transfers between devices, from_everyone(): return lax.all_to_all(copies, axis, split_axis=0, concat_axis=0, tiled=True)  8.03 us
    dot_general x30, matrix products, inverse_root(): lower_part = jnp.matmul(middle, lower_part, precision=lax.Precision.HIGHEST)  8 us
    dot_general x27, matrix products, inverse_root(): upper_part = jnp.matmul(upper_part, middle, precision=lax.Precision.HIGHEST)  7.36 us
    all_to_all x1, starting transfers between devices, from_everyone(): return lax.all_to_all(copies, axis, split_axis=0, concat_axis=0, tiled=True)  5.7 us
    unnamed x18, local copies, waits for them, and re-layouts  5.2 us
    all_to_all x1, starting transfers between devices, sent_and_summed(): lax.all_to_all(in_blocks(array, dim, length), axis, 0, 0, tiled=True)  5.1 us
  transfers between devices with their start and end apart: 3, of which 1 were waited for; matrix products, arithmetic and copies ran while one was open for 17% of the time, Pallas kernels for 0%

profile of v1, /device:TPU:2, one launch (start us, length us, event | category | flops | bytes accessed | tf_op | source)
XLA Modules:
  0.0 163.7 jit_solution(16057323869561955935)
XLA Ops:
  0.6 0.7 copy-done.6
  1.8 1.2 copy.90
  3.0 0.8 copy-done.2
  3.9 0.8 copy-done.3
  4.7 103.0 %environments.1 = (bf16[16,128,128]{2,1,0:T(8,128)(2,1)S(1)}, bf16[2,128,128]{2,1,0:T(8,128)(2,1)S(1)}, bf16[2,128,128]{2,1,0:T(8,128)(2,1)S(1)}) custom-call(s32[2,4,16]{2,1,0:T(4,128)S(1)} %pad_add_fusion.tab, bf16[4,2,128,128]{3,2,1,0:T(8,128)(2,1)S(1)} %bitcast.248, bf16[4,2,128,128]{3,2,1,0:T(8,128)(2,1)S(1)} %bitcast.249, ...), custom_call_target="tpu_custom_call" | custom-call | tf_op jit(solution)/shard_map/environments/pallas_call | solution.py:252
  107.7 0.6 gather_fusion
  108.3 0.3 copy-done.4
  108.6 0.3 copy-done.7
  109.0 0.5 fusion.3
  109.4 0.5 fusion.2
  110.3 1.1 fusion.39
  111.3 1.3 copy.103
  112.7 5.1 %all-to-all-start = ((f32[8,2,128,128]{3,1,2,0:T(2,128)}), f32[8,2,128,128]{3,1,2,0:T(2,128)S(1)}, u32[]{:S(2)}, u32[]{:S(2)}) async-start(f32[8,2,128,128]{3,1,2,0:T(2,128)} %copy.103), calls=%async_computation | async-start | bytes 2097152 | tf_op jit(solution)/shard_map/all_to_all | solution.py:30
  118.6 0.3 fusion.36
  118.9 0.3 fusion.37
  119.2 0.3 multiply_reduce_fusion.1
  119.5 0.3 fusion.25
  119.9 0.3 fusion.69
  128.2 0.3 multiply_reduce_fusion.2
  128.6 0.3 fusion.35
  128.9 0.3 fusion.68
  136.4 0.4 reduce_sum.48
  137.1 0.3 fusion.15
  137.4 0.3 fusion.70
  145.2 0.4 convolution_convert_fusion.4
  145.6 0.9 broadcast_in_dim.43
  146.5 5.7 %all-to-all-start.1 = ((bf16[8,2,128,128]{3,2,1,0:T(8,128)(2,1)}), bf16[8,2,128,128]{3,2,1,0:T(8,128)(2,1)S(1)}, u32[]{:S(2)}, u32[]{:S(2)}) async-start(bf16[8,2,128,128]{3,2,1,0:T(8,128)(2,1)} %broadcast_in_dim.43), calls=%async_computation.1 | async-start | bytes 1048576 | tf_op jit(solution)/shard_map/all_to_all | solution.py:42
  152.5 0.4 fusion.38
  153.2 0.9 copy.109
  154.0 8.0 %all-to-all-done.1 = bf16[8,2,128,128]{3,2,1,0:T(8,128)(2,1)S(1)} async-done(((bf16[8,2,128,128]{3,2,1,0:T(8,128)(2,1)}), bf16[8,2,128,128]{3,2,1,0:T(8,128)(2,1)S(1)}, u32[]{:S(2)}, u32[]{:S(2)}) %all-to-all-start.1) | async-done | bytes 524320 | tf_op jit(solution)/shard_map/all_to_all | solution.py:42
  162.0 0.6 gather_fusion.1
  162.6 1.1 fusion.4
  (114 shorter events, 23.7 us)
Async XLA Ops:
  0.6 0.7 copy-start.6
  1.8 1.2 copy-start
  1.8 1.2 copy-start.1
  3.0 0.8 copy-start.2
  3.9 0.8 copy-start.3
  107.7 1.0 copy-start.4
  108.3 0.7 copy-start.7
  112.7 23.7 %all-to-all-start = ((f32[8,2,128,128]{3,1,2,0:T(2,128)}), f32[8,2,128,128]{3,1,2,0:T(2,128)S(1)}, u32[]{:S(2)}, u32[]{:S(2)}) async-start(f32[8,2,128,128]{3,1,2,0:T(2,128)} %copy.103), calls=%async_computation | async-start | bytes 2097152 | tf_op jit(solution)/shard_map/all_to_all | solution.py:30
  117.8 0.8 copy-start.5
  127.8 17.4 %collective-permute-start = (f32[2,128,128]{2,1,0:T(8,128)S(1)}, f32[2,128,128]{2,1,0:T(8,128)S(1)}, u32[]{:S(2)}, u32[]{:S(2)}) collective-permute-start(f32[2,128,128]{2,1,0:T(8,128)S(1)} %fusion.111), channel_id=1, source_target_pairs={{248,0},{0,8},{8,16},{16,24},{24,32},{32,40},{40,48},{48,56},{56,6... | collective-permute-start | bytes 393224 | tf_op jit(solution)/shard_map/ppermute | solution.py:19
  146.5 15.5 %all-to-all-start.1 = ((bf16[8,2,128,128]{3,2,1,0:T(8,128)(2,1)}), bf16[8,2,128,128]{3,2,1,0:T(8,128)(2,1)S(1)}, u32[]{:S(2)}, u32[]{:S(2)}) async-start(bf16[8,2,128,128]{3,2,1,0:T(8,128)(2,1)} %broadcast_in_dim.43), calls=%async_computation.1 | async-start | bytes 1048576 | tf_op jit(solution)/shard_map/all_to_all | solution.py:42

commit v2 on v1

v2 whole, which is shorter than its diff:
```python
import functools

import jax
import jax.numpy as jnp
from jax import lax
from jax.experimental import pallas as pl
from jax.experimental.pallas import tpu as pltpu
from jax.sharding import PartitionSpec as P

NSI = 10
NAPP = 2
CHUNKS = 4
MESH = pl.DeviceIdType.MESH


def update_kernel(
    sites, secs, steps,
    tab, energy, bond_add, canon_l, canon_r, seed_l, seed_r, site_in, bond_in,
    left_out, right_out,
    own_c, own_s, tall, wab, hold, fresh, pbuf, give, got, nxt, rgt, site_v, bond_v,
    outer, gram_s, gram_r, unit_s, unit_r, fac_s, fac,
    loc_sem, gsend, grecv, ssend, srecv, tsend, trecv, xsend, xrecv,
    usem, osend, orecv, fsend, frecv,
):
    site, sec = lax.axis_index("site"), lax.axis_index("sec")
    role = lax.rem(sec, 2)
    row = sec // 2
    rows = secs // 2
    phys, owned, width = canon_l.shape[0], canon_l.shape[1], canon_l.shape[2]
    sectors = secs * owned
    per = sectors // CHUNKS
    target = lax.rem(site + 1 - 2 * role + sites, sites)
    source = lax.rem(site - 1 + 2 * role + sites, sites)
    peer_sec = row * 2 + 1 - role

    loads = [
        pltpu.make_async_copy(canon_l, own_c.at[0], loc_sem.at[0]),
        pltpu.make_async_copy(canon_r, own_c.at[1], loc_sem.at[1]),
    ]
    center = [
        pltpu.make_async_copy(site_in, site_v, loc_sem.at[2]),
        pltpu.make_async_copy(bond_in, bond_v, loc_sem.at[3]),
    ]
    for load in loads + center:
        load.start()
    for i in range(owned):
        own_s[0, i] = seed_l[i]
        own_s[1, i] = seed_r[i].T

    barrier = pltpu.get_barrier_semaphore()
    others = [(dy, e) for dy in range(rows) for e in range(2) if (dy, e) != (0, 0)]

    def sec_of(dy, e):
        other_role = role + e - 2 * role * e
        return lax.rem(row + dy, rows) * 2 + other_role, other_role

    for dy, e in others:
        pl.semaphore_signal(barrier, inc=1, device_id=(site, sec_of(dy, e)[0]), device_id_type=MESH)
    for other in (target, source):
        pl.semaphore_signal(barrier, inc=1, device_id=(other, sec), device_id_type=MESH)
    pl.semaphore_wait(barrier, len(others) + 2)

    place = pl.ds(sec * owned, owned)
    sent = []
    for n, (dy, e) in enumerate(others):
        to, to_role = sec_of(dy, e)
        sent.append(pltpu.make_async_remote_copy(
            src_ref=own_s.at[to_role], dst_ref=hold.at[0, place],
            send_sem=ssend.at[n], recv_sem=srecv.at[n],
            device_id=(site, to), device_id_type=MESH))
        sent[-1].start()
    for load in loads:
        load.wait()
    keep = [
        pltpu.make_async_copy(own_c.at[role], tall.at[:, place], loc_sem.at[0]),
        pltpu.make_async_copy(own_s.at[role], hold.at[0, place], loc_sem.at[1]),
    ]
    for n, (dy, e) in enumerate(others):
        to, to_role = sec_of(dy, e)
        sent.append(pltpu.make_async_remote_copy(
            src_ref=own_c.at[to_role], dst_ref=tall.at[:, place],
            send_sem=gsend.at[n], recv_sem=grecv.at[n],
            device_id=(site, to), device_id_type=MESH))
        sent[-1].start()
    for copy in keep:
        copy.start()
    for copy in keep:
        copy.wait()
    for copy in sent:
        copy.wait_recv()

    def arrange(i, carry):
        for s in range(phys):
            cols = slice(s * width, (s + 1) * width)
            wab[role, i, :, cols] = tall[s, tab[1, s, i]]
            wab[1 - role, i, :, cols] = tall[s, i].T
        return carry

    lax.fori_loop(0, sectors, arrange, 0)

    def chunk_copy(t, c):
        part = pl.ds(c * per, per)
        return pltpu.make_async_remote_copy(
            src_ref=fresh.at[t, part], dst_ref=hold.at[t + 1, part],
            send_sem=tsend.at[t, c], recv_sem=trecv.at[t, c],
            device_id=(target, sec), device_id_type=MESH)

    def turn(t, carry):
        for c in range(CHUNKS):
            @pl.when(t > 0)
            def _():
                chunk_copy(t - 1, c).wait_recv()

            for i in range(c * per, (c + 1) * per):
                product = jnp.dot(
                    hold[t, i], wab[0, i], preferred_element_type=jnp.float32
                ).astype(jnp.bfloat16)
                for s in range(phys):
                    pbuf[i, s] = product[:, s * width : (s + 1) * width]
        for c in range(CHUNKS):
            for o in range(c * per, (c + 1) * per):
                stack = jnp.concatenate([pbuf[tab[role, s, o], s] for s in range(phys)], axis=0)
                fresh[t, o] = jnp.dot(
                    wab[1, o], stack, preferred_element_type=jnp.float32
                ).astype(jnp.bfloat16)
            chunk_copy(t, c).start()
        return carry

    lax.fori_loop(0, steps, turn, 0)
    for load in center:
        load.wait()

    rows_at = lax.broadcasted_iota(jnp.int32, (width, width), 0)
    cols_at = lax.broadcasted_iota(jnp.int32, (width, width), 1)
    diagonal = rows_at == cols_at
    own_at = sec * owned
    peer_at = peer_sec * owned
    f32, bf16 = jnp.float32, jnp.bfloat16

    def scale_of(ref, t):
        total = ref[t, 0].astype(f32)
        for i in range(1, sectors):
            total = total + ref[t, i].astype(f32)
        return (sectors * width) / jnp.sum(jnp.where(diagonal, total, 0.0))

    def scaled(block, scale):
        return (block.astype(f32) * scale).astype(bf16)

    cur_copies = [pltpu.make_async_remote_copy(
        src_ref=hold.at[steps, pl.ds(c * per, per)], dst_ref=hold.at[steps + 1, pl.ds(c * per, per)],
        send_sem=xsend.at[c], recv_sem=xrecv.at[c],
        device_id=(site, peer_sec), device_id_type=MESH) for c in range(CHUNKS)]
    swap = pltpu.make_async_remote_copy(
        src_ref=give, dst_ref=got,
        send_sem=xsend.at[CHUNKS], recv_sem=xrecv.at[CHUNKS],
        device_id=(site, peer_sec), device_id_type=MESH)

    @pl.when(role == 0)
    def _():
        scale_next = scale_of(fresh, steps - 1)
        for i in range(owned):
            give[i] = scaled(fresh[steps - 1, peer_at + i], scale_next)
        swap.start()
        for i in range(owned):
            nxt[i] = scaled(fresh[steps - 1, own_at + i], scale_next)
        for c in range(CHUNKS):
            chunk_copy(steps - 1, c).wait_recv()
            cur_copies[c].start()
        swap.wait_recv()
        for i in range(owned):
            rgt[i] = got[i].T

    @pl.when(role == 1)
    def _():
        for c in range(CHUNKS):
            chunk_copy(steps - 1, c).wait_recv()
        scale_right = scale_of(hold, steps)
        for i in range(owned):
            give[i] = scaled(hold[steps, peer_at + i], scale_right)
        swap.start()
        for i in range(owned):
            rgt[i] = scaled(hold[steps, own_at + i], scale_right).T
        swap.wait_recv()
        for i in range(owned):
            nxt[i] = got[i]

    def split(x):
        high = x.astype(bf16)
        return high, (x - high.astype(f32)).astype(bf16)

    def as_lhs(parts):
        return jnp.concatenate(parts, axis=1)

    def as_rhs(parts):
        wide = jnp.concatenate(parts, axis=1)
        return jnp.concatenate([wide, wide], axis=0)

    def product(lhs, rhs):
        both = jnp.dot(lhs, rhs, preferred_element_type=f32)
        return both[:, :width] + both[:, width:]

    def middle_of(part):
        return jnp.where(diagonal, 1.5, 0.0) - 0.5 * part

    def inverse_roots(grams):
        norms = [jnp.sqrt(jnp.sum(g * g, keepdims=True)) for g in grams]
        uppers, lowers = [], []
        for g, norm in zip(grams, norms):
            start = g / norm
            middle = middle_of(start)
            uppers.append(product(as_lhs(split(start)), as_rhs(split(middle))))
            lowers.append(middle)

        def repeat(n, carry):
            uppers, lowers = carry
            ups = [split(u) for u in uppers]
            lows = [split(l) for l in lowers]
            mids = [split(middle_of(product(as_lhs(l), as_rhs(u)))) for l, u in zip(lows, ups)]
            return (
                [product(as_lhs(u), as_rhs(m)) for u, m in zip(ups, mids)],
                [product(as_lhs(m), as_rhs(l)) for m, l in zip(mids, lows)],
            )

        uppers, lowers = lax.fori_loop(0, NSI - 2, repeat, (uppers, lowers))
        ups = [split(u) for u in uppers]
        lows = [split(l) for l in lowers]
        mids = [split(middle_of(product(as_lhs(l), as_rhs(u)))) for l, u in zip(lows, ups)]
        return [
            product(as_lhs(m), as_rhs(l)) / jnp.sqrt(norm)
            for m, l, norm in zip(mids, lows, norms)
        ]

    def with_itself(x, dim):
        return lax.dot_general(x, x, (((dim,), (dim,)), ((), ())), preferred_element_type=f32)

    grams = []
    for i in range(owned):
        bond = bond_v[i]
        for repeat in range(NAPP):
            half = jnp.dot(nxt[i], bond, preferred_element_type=f32).astype(bf16)
            bond = (
                jnp.dot(half, rgt[i], preferred_element_type=f32) + bond_add[0] * bond.astype(f32)
            ).astype(bf16)
        bond_v[i] = bond
        grams.append(with_itself(bond, 0))
    for i, root in enumerate(inverse_roots(grams)):
        turned = bond_v[i].T
        unit_s[i] = jnp.dot(
            as_lhs(split(root)), jnp.concatenate([turned, turned], axis=0), preferred_element_type=f32
        )
    unit_copy = pltpu.make_async_remote_copy(
        src_ref=unit_s, dst_ref=unit_r, send_sem=usem.at[0], recv_sem=usem.at[1],
        device_id=(lax.rem(site + 1, sites), sec), device_id_type=MESH)
    unit_copy.start()

    @pl.when(role == 1)
    def _():
        for copy in cur_copies:
            copy.wait_recv()

    scale_cur = scale_of(hold, steps + role)
    for i in range(owned):
        lefts = [scaled(hold[steps + role, tab[0, s, own_at + i]], scale_cur) for s in range(phys)]
        nows = [site_v[s, i] for s in range(phys)]
        for repeat in range(NAPP):
            halves = jnp.concatenate(
                [jnp.dot(l, x, preferred_element_type=f32).astype(bf16) for l, x in zip(lefts, nows)],
                axis=0,
            )
            done = jnp.dot(halves, rgt[i], preferred_element_type=f32)
            nows = [
                (done[s * width : (s + 1) * width] + energy[s] * nows[s].astype(f32)).astype(bf16)
                for s in range(phys)
            ]
        for s in range(phys):
            site_v[s, i] = nows[s]
            outer[s, i] = with_itself(nows[s], 1)

    def pack(d, carry):
        sums = []
        for n in range(owned):
            total = jnp.zeros((width, width), f32)
            for s in range(phys):
                at = tab[1, s, d * owned + n] - own_at
                mine = jnp.logical_and(at >= 0, at < owned)
                block = outer[s, jnp.clip(at, 0, owned - 1)]
                total = total + jnp.where(mine, block, 0.0)
            sums.append(total)
        gram_s[d, :width] = jnp.where(cols_at >= rows_at, sums[0], sums[1])
        line = jnp.sum(jnp.where(diagonal, sums[1], 0.0), axis=0, keepdims=True)
        gram_s[d, width:] = jnp.broadcast_to(line, (8, width))
        return carry

    lax.fori_loop(0, secs, pack, 0)
    gram_copies = []
    for n, (dy, e) in enumerate(others):
        to, _ = sec_of(dy, e)
        gram_copies.append(pltpu.make_async_remote_copy(
            src_ref=gram_s.at[to], dst_ref=gram_r.at[n], send_sem=osend.at[n], recv_sem=orecv.at[n],
            device_id=(site, to), device_id_type=MESH))
        gram_copies[-1].start()

    stacks = [jnp.concatenate([site_v[s, i] for s in range(phys)], axis=0) for i in range(owned)]
    roots = inverse_roots([with_itself(stack, 0) for stack in stacks])
    for i in range(owned):
        factor = product(as_lhs(split(roots[i])), as_rhs(split(unit_s[i]))).astype(bf16)
        stack = jnp.concatenate([site_v[s, i] for s in range(phys)], axis=0)
        fresh_left = jnp.dot(stack, factor, preferred_element_type=f32).astype(bf16)
        for s in range(phys):
            left_out[s, i] = fresh_left[s * width : (s + 1) * width]

    for copy in gram_copies:
        copy.wait_recv()
    total = gram_s[sec]
    for n in range(len(others)):
        total = total + gram_r[n]
    packed, line = total[:width], total[width : width + 1]
    flipped = packed.T
    grams = [
        jnp.where(cols_at >= rows_at, packed, flipped),
        jnp.where(diagonal, line, jnp.where(rows_at > cols_at, packed, flipped)),
    ]
    roots = inverse_roots(grams)
    unit_copy.wait_recv()
    for i in range(owned):
        fac_s[i] = product(as_lhs(split(unit_r[i])), as_rhs(split(roots[i]))).astype(bf16)
    fac_copies = []
    for n, (dy, e) in enumerate(others):
        to, _ = sec_of(dy, e)
        fac_copies.append(pltpu.make_async_remote_copy(
            src_ref=fac_s, dst_ref=fac.at[place], send_sem=fsend.at[n], recv_sem=frecv.at[n],
            device_id=(site, to), device_id_type=MESH))
        fac_copies[-1].start()
    for i in range(owned):
        fac[own_at + i] = fac_s[i]
    for copy in fac_copies:
        copy.wait_recv()
    for i in range(owned):
        for s in range(phys):
            right_out[s, i] = jnp.dot(
                fac[tab[0, s, own_at + i]], site_v[s, i], preferred_element_type=f32
            ).astype(bf16)

    for copy in sent + gram_copies + fac_copies + [swap, unit_copy]:
        copy.wait_send()

    @pl.when(role == 0)
    def _():
        for copy in cur_copies:
            copy.wait_send()

    def drain(t, carry):
        for c in range(CHUNKS):
            chunk_copy(t, c).wait_send()
        return carry

    lax.fori_loop(0, steps, drain, 0)


def update(tables, energy, bond_add, canon_l, canon_r, seed_l, seed_r, site, bond):
    sites, secs = lax.axis_size("site"), lax.axis_size("sec")
    steps = sites // 4
    phys, owned, width = canon_l.shape[:3]
    sectors = owned * secs
    bf16, f32 = jnp.bfloat16, jnp.float32
    block = (width, width)
    dma = pltpu.SemaphoreType.DMA
    smem = pl.BlockSpec(memory_space=pltpu.SMEM)
    vmem = pl.BlockSpec(memory_space=pltpu.VMEM)
    hbm = pl.BlockSpec(memory_space=pl.ANY)
    mail = pltpu.VMEM((secs, width + 8, width), f32)
    return pl.pallas_call(
        functools.partial(update_kernel, sites, secs, steps),
        out_shape=(
            jax.ShapeDtypeStruct((phys, owned, *block), bf16),
            jax.ShapeDtypeStruct((phys, owned, *block), bf16),
        ),
        in_specs=[smem, smem, smem, hbm, hbm, vmem, vmem, hbm, hbm],
        out_specs=(vmem, vmem),
        scratch_shapes=[
            pltpu.VMEM((2, phys, owned, *block), bf16),
            pltpu.VMEM((2, owned, *block), bf16),
            pltpu.VMEM((phys, sectors, *block), bf16),
            pltpu.VMEM((2, sectors, width, phys * width), bf16),
            pltpu.VMEM((steps + 2, sectors, *block), bf16),
            pltpu.VMEM((steps, sectors, *block), bf16),
            pltpu.VMEM((sectors, phys, *block), bf16),
            pltpu.VMEM((owned, *block), bf16),
            pltpu.VMEM((owned, *block), bf16),
            pltpu.VMEM((owned, *block), bf16),
            pltpu.VMEM((owned, *block), bf16),
            pltpu.VMEM((phys, owned, *block), bf16),
            pltpu.VMEM((owned, *block), bf16),
            pltpu.VMEM((phys, owned, *block), f32),
            mail, mail,
            pltpu.VMEM((owned, *block), f32),
            pltpu.VMEM((owned, *block), f32),
            pltpu.VMEM((owned, *block), bf16),
            pltpu.VMEM((sectors, *block), bf16),
            dma((4,)), dma((secs - 1,)), dma((secs - 1,)), dma((secs - 1,)), dma((secs - 1,)),
            dma((steps, CHUNKS)), dma((steps, CHUNKS)), dma((CHUNKS + 1,)), dma((CHUNKS + 1,)),
            dma((2,)), dma((secs - 1,)), dma((secs - 1,)), dma((secs - 1,)), dma((secs - 1,)),
        ],
        compiler_params=pltpu.CompilerParams(
            collective_id=0, has_side_effects=True, vmem_limit_bytes=56 * 1024 * 1024
        ),
        name="environments",
    )(tables, energy, bond_add, canon_l, canon_r, seed_l, seed_r, site, bond)


def per_device(
    left_canon,
    right_canon,
    center_site,
    center_bond,
    left_seed,
    right_seed,
    left_sector,
    onsite,
    bond_shift,
):
    sources = left_sector[0]
    labels = jnp.arange(sources.shape[1], dtype=jnp.int32)
    right_of = jnp.sum(
        jnp.where(sources[:, :, None] == labels[None, None, :], labels[None, :, None], 0), axis=1
    )
    left_new, right_new = update(
        jnp.stack([sources, right_of]), onsite[0], bond_shift, left_canon[0], right_canon[0],
        left_seed[0], right_seed[0], center_site[0], center_bond[0],
    )
    return (left_new[None], right_new[None])


def solution(mesh):
    return jax.shard_map(
        per_device,
        mesh=mesh,
        in_specs=(
            P("site", None, "sec", None, None),
            P("site", None, "sec", None, None),
            P("site", None, "sec", None, None),
            P("site", "sec", None, None),
            P("site", "sec", None, None),
            P("site", "sec", None, None),
            P("site", None, None),
            P("site", None),
            P("site"),
        ),
        out_specs=(P("site", None, "sec", None, None), P("site", None, "sec", None, None)),
        check_vma=False,
    )
```

time: 165 us -> 134 us (0.81)
  matrix products: 29.4 us -> 0 us
  Pallas kernels: 103 us -> 128 us
  starting transfers between devices: 11.1 us -> 0 us
  waiting for transfers between devices: 8.04 us -> 0 us
  local copies, waits for them, and re-layouts: 9.13 us -> 3.09 us
    dot_general x100 -> x0, matrix products: 29.4 us -> none  [the longest x30 8.28 us: inverse_root(): jnp.matmul(lower_part, upper_part, precision=lax.Precision.HIGHEST)]
    pallas_call x1, Pallas kernels: 103 us -> 128 us  [update(): pl.pallas_call(functools.partial(update_kernel, sites, secs, steps), out_...]
    all_to_all x2 -> x0, starting transfers between devices: 10.8 us -> none  [the longest x1 5.7 us: from_everyone(): return lax.all_to_all(copies, axis, split_axis=0, concat_axis=0, tiled=True)]
    all_to_all x2 -> x0, waiting for transfers between devices: 8.03 us -> none  [the longest x1 8.03 us: from_everyone(): return lax.all_to_all(copies, axis, split_axis=0, concat_axis=0, tiled=True)]
    unnamed x18 -> x6, local copies, waits for them, and re-layouts: 5.2 us -> 3.09 us
  transfers between devices with their start and end apart: 3 -> 0, of which waited for: 1 -> 0; matrix products, arithmetic and copies ran while one was open for 17% -> 0% of each run, Pallas kernels for 0% -> 0%
where the time goes in v2:
time: 134 us; the launch traced here: 133 us
  Pallas kernels  128 us (96%)
  local copies, waits for them, and re-layouts  3.09 us (2%)
    pallas_call x1, Pallas kernels, update(): pl.pallas_call(functools.partial(update_kernel, sites, secs, steps), out_...  128 us
    unnamed x6, local copies, waits for them, and re-layouts  3.09 us

profile of v2, /device:TPU:2, one launch (start us, length us, event | category | flops | bytes accessed | tf_op | source)
XLA Modules:
  0.0 132.7 jit_solution(10370098455309702239)
XLA Ops:
  1.3 0.0 copy-start.1
  1.3 0.7 copy-done.1
  2.0 0.1 select_reduce_fusion
  2.1 0.6 pad_add_fusion.tab
  2.7 127.6 %environments.1 = (bf16[4,2,128,128]{3,2,1,0:T(8,128)(2,1)}, bf16[4,2,128,128]{3,2,1,0:T(8,128)(2,1)}) custom-call(s32[2,4,16]{2,1,0:T(4,128)} %pad_add_fusion.tab, f32[4]{0:T(128)} %bitcast.21, f32[1]{0:T(128)S(6)} %copy.13.bond_add, bf16[4,2,128,128]{3,2,1,0:T(8,128)(2,1)} %bitcast.11, bf16[4,2,128,128]{3,2,1,0:T(8,128)(2,1)} %bitcast.12, ...), custom_call_target="tpu_custom_call" | custom-call | tf_op jit(solution)/shard_map/environments/pallas_call | solution.py:372
  130.2 0.0 copy-start
  130.3 1.7 %copy.14 = bf16[1,4,2,128,128]{4,3,2,1,0:T(8,128)(2,1)} copy(bf16[1,4,2,128,128]{4,3,2,1,0:T(8,128)(2,1)} %bitcast.15) | data formatting | bytes 524288
  132.0 0.0 copy-done
  132.0 0.7 copy.15
Async XLA Ops:
  1.3 0.7 copy-start.1
  130.2 1.7 %copy-start = (bf16[4,2,128,128]{3,2,1,0:T(8,128)(2,1)S(1)}, bf16[4,2,128,128]{3,2,1,0:T(8,128)(2,1)}, u32[]{:S(2)}) copy-start(bf16[4,2,128,128]{3,2,1,0:T(8,128)(2,1)} %get-tuple-element.5) | copy-start | bytes 786436

commit v3 on v2

--- a/solution.py
+++ b/solution.py
@@ -9,7 +9,7 @@
 
 NSI = 10
 NAPP = 2
-CHUNKS = 4
+CHUNKS = (3, 3, 4, 3, 3)
 MESH = pl.DeviceIdType.MESH
 
 
@@ -17,10 +17,10 @@
     sites, secs, steps,
     tab, energy, bond_add, canon_l, canon_r, seed_l, seed_r, site_in, bond_in,
     left_out, right_out,
-    own_c, own_s, tall, wab, hold, fresh, pbuf, give, got, nxt, rgt, site_v, bond_v,
+    own_c, own_s, tall, wab, hold, fresh, pbuf, give_n, got_n, give_r, got_r, nxt, rgt, site_v, bond_v,
     outer, gram_s, gram_r, unit_s, unit_r, fac_s, fac,
     loc_sem, gsend, grecv, ssend, srecv, tsend, trecv, xsend, xrecv,
-    usem, osend, orecv, fsend, frecv,
+    usem, osend, orecv, fsend, frecv, psend, rsend, rrecv,
 ):
     site, sec = lax.axis_index("site"), lax.axis_index("sec")
     role = lax.rem(sec, 2)
@@ -28,10 +28,19 @@
     rows = secs // 2
     phys, owned, width = canon_l.shape[0], canon_l.shape[1], canon_l.shape[2]
     sectors = secs * owned
-    per = sectors // CHUNKS
     target = lax.rem(site + 1 - 2 * role + sites, sites)
     source = lax.rem(site - 1 + 2 * role + sites, sites)
     peer_sec = row * 2 + 1 - role
+    half = lax.rem(row, 2)
+    pair_sec = sec + 2 - 4 * half
+    far_target = lax.rem(site, 2) != role
+    far_source = lax.rem(site, 2) == role
+    ends = sectors - CHUNKS[0] - CHUNKS[1]
+    starts = (
+        half * ends, half * ends + CHUNKS[0], CHUNKS[0] + CHUNKS[1],
+        (1 - half) * ends, (1 - half) * ends + CHUNKS[0],
+    )
+    last = steps - 1
 
     loads = [
         pltpu.make_async_copy(canon_l, own_c.at[0], loc_sem.at[0]),
@@ -58,7 +67,9 @@
         pl.semaphore_signal(barrier, inc=1, device_id=(site, sec_of(dy, e)[0]), device_id_type=MESH)
     for other in (target, source):
         pl.semaphore_signal(barrier, inc=1, device_id=(other, sec), device_id_type=MESH)
-    pl.semaphore_wait(barrier, len(others) + 2)
+    across = lax.rem(site + 1 - 2 * role + sites, sites)
+    pl.semaphore_signal(barrier, inc=1, device_id=(across, peer_sec), device_id_type=MESH)
+    pl.semaphore_wait(barrier, len(others) + 3)
 
     place = pl.ds(sec * owned, owned)
     sent = []
@@ -99,34 +110,71 @@
     lax.fori_loop(0, sectors, arrange, 0)
 
     def chunk_copy(t, c):
-        part = pl.ds(c * per, per)
+        part = pl.ds(starts[c], CHUNKS[c])
         return pltpu.make_async_remote_copy(
             src_ref=fresh.at[t, part], dst_ref=hold.at[t + 1, part],
             send_sem=tsend.at[t, c], recv_sem=trecv.at[t, c],
             device_id=(target, sec), device_id_type=MESH)
 
-    def turn(t, carry):
-        for c in range(CHUNKS):
+    def pair_copy(t, c):
+        part = pl.ds(starts[c], CHUNKS[c])
+        return pltpu.make_async_remote_copy(
+            src_ref=hold.at[t + 1, part], dst_ref=hold.at[t + 1, part],
+            send_sem=psend.at[t, c], recv_sem=trecv.at[t, c + 3],
+            device_id=(site, pair_sec), device_id_type=MESH)
+
+    def arrive(t, c):
+        chunk_copy(t, c).wait_recv()
+        if c < 2:
+            @pl.when(far_source)
+            def _():
+                pair_copy(t, c).start()
+
+    def first_half(t):
+        for c, length in enumerate(CHUNKS):
             @pl.when(t > 0)
             def _():
-                chunk_copy(t - 1, c).wait_recv()
-
-            for i in range(c * per, (c + 1) * per):
+                arrive(t - 1, c)
+
+            for i in range(length):
+                at = starts[c] + i
                 product = jnp.dot(
-                    hold[t, i], wab[0, i], preferred_element_type=jnp.float32
+                    hold[t, at], wab[0, at], preferred_element_type=jnp.float32
                 ).astype(jnp.bfloat16)
                 for s in range(phys):
-                    pbuf[i, s] = product[:, s * width : (s + 1) * width]
-        for c in range(CHUNKS):
-            for o in range(c * per, (c + 1) * per):
-                stack = jnp.concatenate([pbuf[tab[role, s, o], s] for s in range(phys)], axis=0)
-                fresh[t, o] = jnp.dot(
-                    wab[1, o], stack, preferred_element_type=jnp.float32
+                    pbuf[at, s] = product[:, s * width : (s + 1) * width]
+
+    def second_half(t, send):
+        for c, length in enumerate(CHUNKS):
+            for i in range(length):
+                at = starts[c] + i
+                stack = jnp.concatenate([pbuf[tab[role, s, at], s] for s in range(phys)], axis=0)
+                fresh[t, at] = jnp.dot(
+                    wab[1, at], stack, preferred_element_type=jnp.float32
                 ).astype(jnp.bfloat16)
+            send(t, c)
+
+    def send_on(t, c):
+        if c < 3:
             chunk_copy(t, c).start()
+        else:
+            @pl.when(jnp.logical_not(far_target))
+            def _():
+                chunk_copy(t, c).start()
+
+    def send_left(t, c):
+        @pl.when(role == 0)
+        def _():
+            send_on(t, c)
+
+    def turn(t, carry):
+        first_half(t)
+        second_half(t, send_on)
         return carry
 
-    lax.fori_loop(0, steps, turn, 0)
+    lax.fori_loop(0, last, turn, 0)
+    first_half(last)
+    second_half(last, send_left)
     for load in center:
         load.wait()
 
@@ -147,42 +195,45 @@
         return (block.astype(f32) * scale).astype(bf16)
 
     cur_copies = [pltpu.make_async_remote_copy(
-        src_ref=hold.at[steps, pl.ds(c * per, per)], dst_ref=hold.at[steps + 1, pl.ds(c * per, per)],
+        src_ref=hold.at[steps, pl.ds(starts[c], CHUNKS[c])],
+        dst_ref=hold.at[steps + 1, pl.ds(starts[c], CHUNKS[c])],
         send_sem=xsend.at[c], recv_sem=xrecv.at[c],
-        device_id=(site, peer_sec), device_id_type=MESH) for c in range(CHUNKS)]
-    swap = pltpu.make_async_remote_copy(
-        src_ref=give, dst_ref=got,
-        send_sem=xsend.at[CHUNKS], recv_sem=xrecv.at[CHUNKS],
+        device_id=(site, peer_sec), device_id_type=MESH) for c in range(len(CHUNKS))]
+    nxt_copy = pltpu.make_async_remote_copy(
+        src_ref=give_n, dst_ref=got_n,
+        send_sem=xsend.at[len(CHUNKS)], recv_sem=xrecv.at[len(CHUNKS)],
         device_id=(site, peer_sec), device_id_type=MESH)
+    rgt_copies = [pltpu.make_async_remote_copy(
+        src_ref=give_r.at[n], dst_ref=got_r,
+        send_sem=rsend.at[n], recv_sem=rrecv.at[0],
+        device_id=(target, to), device_id_type=MESH) for n, to in enumerate((peer_sec, sec))]
 
     @pl.when(role == 0)
     def _():
-        scale_next = scale_of(fresh, steps - 1)
+        scale_next = scale_of(fresh, last)
         for i in range(owned):
-            give[i] = scaled(fresh[steps - 1, peer_at + i], scale_next)
-        swap.start()
+            give_n[i] = scaled(fresh[last, peer_at + i], scale_next)
+        nxt_copy.start()
         for i in range(owned):
-            nxt[i] = scaled(fresh[steps - 1, own_at + i], scale_next)
-        for c in range(CHUNKS):
-            chunk_copy(steps - 1, c).wait_recv()
+            nxt[i] = scaled(fresh[last, own_at + i], scale_next)
+        for c in range(len(CHUNKS)):
+            arrive(last, c)
             cur_copies[c].start()
-        swap.wait_recv()
-        for i in range(owned):
-            rgt[i] = got[i].T
 
     @pl.when(role == 1)
     def _():
-        for c in range(CHUNKS):
-            chunk_copy(steps - 1, c).wait_recv()
-        scale_right = scale_of(hold, steps)
+        scale_right = scale_of(fresh, last)
+        for n, start in enumerate((peer_at, own_at)):
+            for i in range(owned):
+                give_r[n, i] = scaled(fresh[last, start + i], scale_right)
+            rgt_copies[n].start()
+        nxt_copy.wait_recv()
         for i in range(owned):
-            give[i] = scaled(hold[steps, peer_at + i], scale_right)
-        swap.start()
-        for i in range(owned):
-            rgt[i] = scaled(hold[steps, own_at + i], scale_right).T
-        swap.wait_recv()
-        for i in range(owned):
-            nxt[i] = got[i]
+            nxt[i] = got_n[i]
+
+    rgt_copies[0].wait_recv()
+    for i in range(owned):
+        rgt[i] = got_r[i].T
 
     def split(x):
         high = x.astype(bf16)
@@ -341,20 +392,38 @@
                 fac[tab[0, s, own_at + i]], site_v[s, i], preferred_element_type=f32
             ).astype(bf16)
 
-    for copy in sent + gram_copies + fac_copies + [swap, unit_copy]:
+    for copy in sent + gram_copies + fac_copies + [unit_copy]:
         copy.wait_send()
+
+    def drain(t, carry):
+        for c in range(3):
+            chunk_copy(t, c).wait_send()
+
+        @pl.when(jnp.logical_not(far_target))
+        def _():
+            for c in range(3, len(CHUNKS)):
+                chunk_copy(t, c).wait_send()
+
+        @pl.when(far_source)
+        def _():
+            for c in range(2):
+                pair_copy(t, c).wait_send()
+
+        return carry
+
+    lax.fori_loop(0, last, drain, 0)
 
     @pl.when(role == 0)
     def _():
+        drain(last, 0)
+        nxt_copy.wait_send()
         for copy in cur_copies:
             copy.wait_send()
 
-    def drain(t, carry):
-        for c in range(CHUNKS):
-            chunk_copy(t, c).wait_send()
-        return carry
-
-    lax.fori_loop(0, steps, drain, 0)
+    @pl.when(role == 1)
+    def _():
+        for copy in rgt_copies:
+            copy.wait_send()
 
 
 def update(tables, energy, bond_add, canon_l, canon_r, seed_l, seed_r, site, bond):
@@ -387,6 +456,8 @@
             pltpu.VMEM((sectors, phys, *block), bf16),
             pltpu.VMEM((owned, *block), bf16),
             pltpu.VMEM((owned, *block), bf16),
+            pltpu.VMEM((2, owned, *block), bf16),
+            pltpu.VMEM((owned, *block), bf16),
             pltpu.VMEM((owned, *block), bf16),
             pltpu.VMEM((owned, *block), bf16),
             pltpu.VMEM((phys, owned, *block), bf16),
@@ -398,8 +469,10 @@
             pltpu.VMEM((owned, *block), bf16),
             pltpu.VMEM((sectors, *block), bf16),
             dma((4,)), dma((secs - 1,)), dma((secs - 1,)), dma((secs - 1,)), dma((secs - 1,)),
-            dma((steps, CHUNKS)), dma((steps, CHUNKS)), dma((CHUNKS + 1,)), dma((CHUNKS + 1,)),
+            dma((steps, len(CHUNKS))), dma((steps, len(CHUNKS))),
+            dma((len(CHUNKS) + 1,)), dma((len(CHUNKS) + 1,)),
             dma((2,)), dma((secs - 1,)), dma((secs - 1,)), dma((secs - 1,)), dma((secs - 1,)),
+            dma((steps, 2)), dma((2,)), dma((1,)),
         ],
         compiler_params=pltpu.CompilerParams(
             collective_id=0, has_side_effects=True, vmem_limit_bytes=56 * 1024 * 1024

time: 134 us -> 135 us (level)
    pallas_call x1, Pallas kernels: 128 us -> 129 us  [update(): pl.pallas_call(functools.partial(update_kernel, sites, secs, steps), out_...]
where the time goes in v3:
time: 135 us; the launch traced here: 134 us
  Pallas kernels  129 us (96%)
  local copies, waits for them, and re-layouts  3.09 us (2%)
    pallas_call x1, Pallas kernels, update(): pl.pallas_call(functools.partial(update_kernel, sites, secs, steps), out_...  129 us
    unnamed x6, local copies, waits for them, and re-layouts  3.09 us

profile of v3, /device:TPU:2, one launch (start us, length us, event | category | flops | bytes accessed | tf_op | source)
XLA Modules:
  0.0 134.3 jit_solution(15364021532865978556)
XLA Ops:
  1.3 0.0 copy-start.1
  1.3 0.7 copy-done.1
  2.0 0.1 select_reduce_fusion
  2.1 0.6 pad_add_fusion.tab
  2.7 129.2 %environments.1 = (bf16[4,2,128,128]{3,2,1,0:T(8,128)(2,1)}, bf16[4,2,128,128]{3,2,1,0:T(8,128)(2,1)}) custom-call(s32[2,4,16]{2,1,0:T(4,128)} %pad_add_fusion.tab, f32[4]{0:T(128)} %bitcast.21, f32[1]{0:T(128)S(6)} %copy.13.bond_add, bf16[4,2,128,128]{3,2,1,0:T(8,128)(2,1)} %bitcast.11, bf16[4,2,128,128]{3,2,1,0:T(8,128)(2,1)} %bitcast.12, ...), custom_call_target="tpu_custom_call" | custom-call | tf_op jit(solution)/shard_map/environments/pallas_call | solution.py:441
  131.9 0.0 copy-start
  131.9 1.7 %copy.14 = bf16[1,4,2,128,128]{4,3,2,1,0:T(8,128)(2,1)} copy(bf16[1,4,2,128,128]{4,3,2,1,0:T(8,128)(2,1)} %bitcast.15) | data formatting | bytes 524288
  133.6 0.0 copy-done
  133.6 0.7 copy.15
Async XLA Ops:
  1.3 0.7 copy-start.1
  131.9 1.7 %copy-start = (bf16[4,2,128,128]{3,2,1,0:T(8,128)(2,1)S(1)}, bf16[4,2,128,128]{3,2,1,0:T(8,128)(2,1)}, u32[]{:S(2)}) copy-start(bf16[4,2,128,128]{3,2,1,0:T(8,128)(2,1)} %get-tuple-element.5) | copy-start | bytes 786436

commit v4 on v3

--- a/solution.py
+++ b/solution.py
@@ -9,7 +9,8 @@
 
 NSI = 10
 NAPP = 2
-CHUNKS = (3, 3, 4, 3, 3)
+NEAR = (8, 8)
+FAR = (3, 5, 5, 3)
 MESH = pl.DeviceIdType.MESH
 
 
@@ -17,7 +18,7 @@
     sites, secs, steps,
     tab, energy, bond_add, canon_l, canon_r, seed_l, seed_r, site_in, bond_in,
     left_out, right_out,
-    own_c, own_s, tall, wab, hold, fresh, pbuf, give_n, got_n, give_r, got_r, nxt, rgt, site_v, bond_v,
+    own_c, own_s, tall, wab, hold, fresh, pbuf, give_n, got_n, give_r, got_r, give_c, lefts, nxt, rgt, site_v, bond_v,
     outer, gram_s, gram_r, unit_s, unit_r, fac_s, fac,
     loc_sem, gsend, grecv, ssend, srecv, tsend, trecv, xsend, xrecv,
     usem, osend, orecv, fsend, frecv, psend, rsend, rrecv,
@@ -35,11 +36,9 @@
     pair_sec = sec + 2 - 4 * half
     far_target = lax.rem(site, 2) != role
     far_source = lax.rem(site, 2) == role
-    ends = sectors - CHUNKS[0] - CHUNKS[1]
-    starts = (
-        half * ends, half * ends + CHUNKS[0], CHUNKS[0] + CHUNKS[1],
-        (1 - half) * ends, (1 - half) * ends + CHUNKS[0],
-    )
+    ends = sectors - FAR[0]
+    far_at = (half * ends, FAR[0], FAR[0] + FAR[1], (1 - half) * ends)
+    near_at = (0, NEAR[0])
     last = steps - 1
 
     loads = [
@@ -109,67 +108,87 @@
 
     lax.fori_loop(0, sectors, arrange, 0)
 
-    def chunk_copy(t, c):
-        part = pl.ds(starts[c], CHUNKS[c])
+    def to_target(t, c, part):
         return pltpu.make_async_remote_copy(
             src_ref=fresh.at[t, part], dst_ref=hold.at[t + 1, part],
             send_sem=tsend.at[t, c], recv_sem=trecv.at[t, c],
             device_id=(target, sec), device_id_type=MESH)
 
-    def pair_copy(t, c):
-        part = pl.ds(starts[c], CHUNKS[c])
+    def far_copy(t, c):
+        return to_target(t, c, pl.ds(far_at[c], FAR[c]))
+
+    def near_copy(t, c):
+        return to_target(t, c, pl.ds(near_at[c], NEAR[c]))
+
+    def pair_copy(t):
+        part = pl.ds(far_at[0], FAR[0])
         return pltpu.make_async_remote_copy(
             src_ref=hold.at[t + 1, part], dst_ref=hold.at[t + 1, part],
-            send_sem=psend.at[t, c], recv_sem=trecv.at[t, c + 3],
+            send_sem=psend.at[t], recv_sem=trecv.at[t, 3],
             device_id=(site, pair_sec), device_id_type=MESH)
 
-    def arrive(t, c):
-        chunk_copy(t, c).wait_recv()
-        if c < 2:
-            @pl.when(far_source)
-            def _():
-                pair_copy(t, c).start()
+    def apply_right(t, start, length):
+        for i in range(length):
+            at = start + i
+            product = jnp.dot(
+                hold[t, at], wab[0, at], preferred_element_type=jnp.float32
+            ).astype(jnp.bfloat16)
+            for s in range(phys):
+                pbuf[at, s] = product[:, s * width : (s + 1) * width]
+
+    def apply_left(t, start, length):
+        for i in range(length):
+            at = start + i
+            stack = jnp.concatenate([pbuf[tab[role, s, at], s] for s in range(phys)], axis=0)
+            fresh[t, at] = jnp.dot(
+                wab[1, at], stack, preferred_element_type=jnp.float32
+            ).astype(jnp.bfloat16)
 
     def first_half(t):
-        for c, length in enumerate(CHUNKS):
+        came_far = jnp.logical_and(t > 0, far_source)
+
+        @pl.when(came_far)
+        def _():
+            far_copy(t - 1, 0).wait_recv()
+            pair_copy(t - 1).start()
+            far_copy(t - 1, 1).wait_recv()
+            apply_right(t, far_at[0], FAR[0])
+            apply_right(t, far_at[1], FAR[1])
+            for c in (2, 3):
+                far_copy(t - 1, c).wait_recv()
+                apply_right(t, far_at[c], FAR[c])
+
+        @pl.when(jnp.logical_not(came_far))
+        def _():
             @pl.when(t > 0)
             def _():
-                arrive(t - 1, c)
-
-            for i in range(length):
-                at = starts[c] + i
-                product = jnp.dot(
-                    hold[t, at], wab[0, at], preferred_element_type=jnp.float32
-                ).astype(jnp.bfloat16)
-                for s in range(phys):
-                    pbuf[at, s] = product[:, s * width : (s + 1) * width]
+                for c in range(len(NEAR)):
+                    near_copy(t - 1, c).wait_recv()
+
+            apply_right(t, 0, sectors)
 
     def second_half(t, send):
-        for c, length in enumerate(CHUNKS):
-            for i in range(length):
-                at = starts[c] + i
-                stack = jnp.concatenate([pbuf[tab[role, s, at], s] for s in range(phys)], axis=0)
-                fresh[t, at] = jnp.dot(
-                    wab[1, at], stack, preferred_element_type=jnp.float32
-                ).astype(jnp.bfloat16)
-            send(t, c)
-
-    def send_on(t, c):
-        if c < 3:
-            chunk_copy(t, c).start()
-        else:
-            @pl.when(jnp.logical_not(far_target))
-            def _():
-                chunk_copy(t, c).start()
-
-    def send_left(t, c):
+        @pl.when(far_target)
+        def _():
+            for c in range(3):
+                apply_left(t, far_at[c], FAR[c])
+                send(far_copy(t, c))
+            apply_left(t, far_at[3], FAR[3])
+
+        @pl.when(jnp.logical_not(far_target))
+        def _():
+            for c in range(len(NEAR)):
+                apply_left(t, near_at[c], NEAR[c])
+                send(near_copy(t, c))
+
+    def send_left(copy):
         @pl.when(role == 0)
         def _():
-            send_on(t, c)
+            copy.start()
 
     def turn(t, carry):
         first_half(t)
-        second_half(t, send_on)
+        second_half(t, lambda copy: copy.start())
         return carry
 
     lax.fori_loop(0, last, turn, 0)
@@ -194,14 +213,12 @@
     def scaled(block, scale):
         return (block.astype(f32) * scale).astype(bf16)
 
-    cur_copies = [pltpu.make_async_remote_copy(
-        src_ref=hold.at[steps, pl.ds(starts[c], CHUNKS[c])],
-        dst_ref=hold.at[steps + 1, pl.ds(starts[c], CHUNKS[c])],
-        send_sem=xsend.at[c], recv_sem=xrecv.at[c],
-        device_id=(site, peer_sec), device_id_type=MESH) for c in range(len(CHUNKS))]
+    cur_copy = pltpu.make_async_remote_copy(
+        src_ref=give_c, dst_ref=lefts, send_sem=xsend.at[0], recv_sem=xrecv.at[0],
+        device_id=(site, peer_sec), device_id_type=MESH)
     nxt_copy = pltpu.make_async_remote_copy(
         src_ref=give_n, dst_ref=got_n,
-        send_sem=xsend.at[len(CHUNKS)], recv_sem=xrecv.at[len(CHUNKS)],
+        send_sem=xsend.at[1], recv_sem=xrecv.at[1],
         device_id=(site, peer_sec), device_id_type=MESH)
     rgt_copies = [pltpu.make_async_remote_copy(
         src_ref=give_r.at[n], dst_ref=got_r,
@@ -216,9 +233,27 @@
         nxt_copy.start()
         for i in range(owned):
             nxt[i] = scaled(fresh[last, own_at + i], scale_next)
-        for c in range(len(CHUNKS)):
-            arrive(last, c)
-            cur_copies[c].start()
+
+        @pl.when(far_source)
+        def _():
+            for c in range(4):
+                far_copy(last, c).wait_recv()
+                if c == 0:
+                    pair_copy(last).start()
+
+        @pl.when(jnp.logical_not(far_source))
+        def _():
+            for c in range(len(NEAR)):
+                near_copy(last, c).wait_recv()
+
+        scale_cur = scale_of(hold, steps)
+        for i in range(owned):
+            for s in range(phys):
+                give_c[s, i] = scaled(hold[steps, tab[0, s, peer_at + i]], scale_cur)
+        cur_copy.start()
+        for i in range(owned):
+            for s in range(phys):
+                lefts[s, i] = scaled(hold[steps, tab[0, s, own_at + i]], scale_cur)
 
     @pl.when(role == 1)
     def _():
@@ -306,16 +341,16 @@
 
     @pl.when(role == 1)
     def _():
-        for copy in cur_copies:
-            copy.wait_recv()
-
-    scale_cur = scale_of(hold, steps + role)
-    for i in range(owned):
-        lefts = [scaled(hold[steps + role, tab[0, s, own_at + i]], scale_cur) for s in range(phys)]
+        cur_copy.wait_recv()
+
+    for i in range(owned):
         nows = [site_v[s, i] for s in range(phys)]
         for repeat in range(NAPP):
             halves = jnp.concatenate(
-                [jnp.dot(l, x, preferred_element_type=f32).astype(bf16) for l, x in zip(lefts, nows)],
+                [
+                    jnp.dot(lefts[s, i], nows[s], preferred_element_type=f32).astype(bf16)
+                    for s in range(phys)
+                ],
                 axis=0,
             )
             done = jnp.dot(halves, rgt[i], preferred_element_type=f32)
@@ -327,12 +362,18 @@
             site_v[s, i] = nows[s]
             outer[s, i] = with_itself(nows[s], 1)
 
-    def pack(d, carry):
+    def gram_copy(d):
+        return pltpu.make_async_remote_copy(
+            src_ref=gram_s.at[d], dst_ref=gram_r.at[sec], send_sem=osend.at[d], recv_sem=orecv.at[sec],
+            device_id=(site, d), device_id_type=MESH)
+
+    def pack(n, carry):
+        d = lax.rem(sec + 1 + n, secs)
         sums = []
-        for n in range(owned):
+        for i in range(owned):
             total = jnp.zeros((width, width), f32)
             for s in range(phys):
-                at = tab[1, s, d * owned + n] - own_at
+                at = tab[1, s, d * owned + i] - own_at
                 mine = jnp.logical_and(at >= 0, at < owned)
                 block = outer[s, jnp.clip(at, 0, owned - 1)]
                 total = total + jnp.where(mine, block, 0.0)
@@ -340,16 +381,14 @@
         gram_s[d, :width] = jnp.where(cols_at >= rows_at, sums[0], sums[1])
         line = jnp.sum(jnp.where(diagonal, sums[1], 0.0), axis=0, keepdims=True)
         gram_s[d, width:] = jnp.broadcast_to(line, (8, width))
+
+        @pl.when(n < secs - 1)
+        def _():
+            gram_copy(d).start()
+
         return carry
 
     lax.fori_loop(0, secs, pack, 0)
-    gram_copies = []
-    for n, (dy, e) in enumerate(others):
-        to, _ = sec_of(dy, e)
-        gram_copies.append(pltpu.make_async_remote_copy(
-            src_ref=gram_s.at[to], dst_ref=gram_r.at[n], send_sem=osend.at[n], recv_sem=orecv.at[n],
-            device_id=(site, to), device_id_type=MESH))
-        gram_copies[-1].start()
 
     stacks = [jnp.concatenate([site_v[s, i] for s in range(phys)], axis=0) for i in range(owned)]
     roots = inverse_roots([with_itself(stack, 0) for stack in stacks])
@@ -360,11 +399,16 @@
         for s in range(phys):
             left_out[s, i] = fresh_left[s * width : (s + 1) * width]
 
-    for copy in gram_copies:
-        copy.wait_recv()
+    def gram_from(d):
+        return pltpu.make_async_remote_copy(
+            src_ref=gram_s.at[d], dst_ref=gram_r.at[d], send_sem=osend.at[d], recv_sem=orecv.at[d],
+            device_id=(site, d), device_id_type=MESH)
+
+    for n in range(secs - 1):
+        gram_from(lax.rem(sec + 1 + n, secs)).wait_recv()
     total = gram_s[sec]
-    for n in range(len(others)):
-        total = total + gram_r[n]
+    for n in range(secs - 1):
+        total = total + gram_r[lax.rem(sec + 1 + n, secs)]
     packed, line = total[:width], total[width : width + 1]
     flipped = packed.T
     grams = [
@@ -392,22 +436,25 @@
                 fac[tab[0, s, own_at + i]], site_v[s, i], preferred_element_type=f32
             ).astype(bf16)
 
-    for copy in sent + gram_copies + fac_copies + [unit_copy]:
+    for copy in sent + fac_copies + [unit_copy]:
         copy.wait_send()
+    for n in range(secs - 1):
+        gram_copy(lax.rem(sec + 1 + n, secs)).wait_send()
 
     def drain(t, carry):
-        for c in range(3):
-            chunk_copy(t, c).wait_send()
+        @pl.when(far_target)
+        def _():
+            for c in range(3):
+                far_copy(t, c).wait_send()
 
         @pl.when(jnp.logical_not(far_target))
         def _():
-            for c in range(3, len(CHUNKS)):
-                chunk_copy(t, c).wait_send()
+            for c in range(len(NEAR)):
+                near_copy(t, c).wait_send()
 
         @pl.when(far_source)
         def _():
-            for c in range(2):
-                pair_copy(t, c).wait_send()
+            pair_copy(t).wait_send()
 
         return carry
 
@@ -417,8 +464,7 @@
     def _():
         drain(last, 0)
         nxt_copy.wait_send()
-        for copy in cur_copies:
-            copy.wait_send()
+        cur_copy.wait_send()
 
     @pl.when(role == 1)
     def _():
@@ -451,13 +497,15 @@
             pltpu.VMEM((2, owned, *block), bf16),
             pltpu.VMEM((phys, sectors, *block), bf16),
             pltpu.VMEM((2, sectors, width, phys * width), bf16),
-            pltpu.VMEM((steps + 2, sectors, *block), bf16),
+            pltpu.VMEM((steps + 1, sectors, *block), bf16),
             pltpu.VMEM((steps, sectors, *block), bf16),
             pltpu.VMEM((sectors, phys, *block), bf16),
             pltpu.VMEM((owned, *block), bf16),
             pltpu.VMEM((owned, *block), bf16),
             pltpu.VMEM((2, owned, *block), bf16),
             pltpu.VMEM((owned, *block), bf16),
+            pltpu.VMEM((phys, owned, *block), bf16),
+            pltpu.VMEM((phys, owned, *block), bf16),
             pltpu.VMEM((owned, *block), bf16),
             pltpu.VMEM((owned, *block), bf16),
             pltpu.VMEM((phys, owned, *block), bf16),
@@ -469,10 +517,9 @@
             pltpu.VMEM((owned, *block), bf16),
             pltpu.VMEM((sectors, *block), bf16),
             dma((4,)), dma((secs - 1,)), dma((secs - 1,)), dma((secs - 1,)), dma((secs - 1,)),
-            dma((steps, len(CHUNKS))), dma((steps, len(CHUNKS))),
-            dma((len(CHUNKS) + 1,)), dma((len(CHUNKS) + 1,)),
-            dma((2,)), dma((secs - 1,)), dma((secs - 1,)), dma((secs - 1,)), dma((secs - 1,)),
-            dma((steps, 2)), dma((2,)), dma((1,)),
+            dma((steps, 4)), dma((steps, 4)), dma((2,)), dma((2,)),
+            dma((2,)), dma((secs,)), dma((secs,)), dma((secs - 1,)), dma((secs - 1,)),
+            dma((steps,)), dma((2,)), dma((1,)),
         ],
         compiler_params=pltpu.CompilerParams(
             collective_id=0, has_side_effects=True, vmem_limit_bytes=56 * 1024 * 1024

time: 135 us -> 121 us (0.90)
  Pallas kernels: 129 us -> 114 us
    pallas_call x1, Pallas kernels: 129 us -> 114 us  [update(): pl.pallas_call(functools.partial(update_kernel, sites, secs, steps), out_...]
where the time goes in v4:
time: 121 us; the launch traced here: 119 us
  Pallas kernels  114 us (94%)
  local copies, waits for them, and re-layouts  3.09 us (3%)
  between operations  1.3 us (1%)
    pallas_call x1, Pallas kernels, update(): pl.pallas_call(functools.partial(update_kernel, sites, secs, steps), out_...  114 us
    unnamed x6, local copies, waits for them, and re-layouts  3.09 us

profile of v4, /device:TPU:2, one launch (start us, length us, event | category | flops | bytes accessed | tf_op | source)
XLA Modules:
  0.0 119.5 jit_solution(13927691649487086415)
XLA Ops:
  1.3 0.0 copy-start.1
  1.3 0.7 copy-done.1
  2.0 0.1 select_reduce_fusion
  2.1 0.6 pad_add_fusion.tab
  2.7 114.4 %environments.1 = (bf16[4,2,128,128]{3,2,1,0:T(8,128)(2,1)}, bf16[4,2,128,128]{3,2,1,0:T(8,128)(2,1)}) custom-call(s32[2,4,16]{2,1,0:T(4,128)} %pad_add_fusion.tab, f32[4]{0:T(128)} %bitcast.21, f32[1]{0:T(128)S(6)} %copy.13.bond_add, bf16[4,2,128,128]{3,2,1,0:T(8,128)(2,1)} %bitcast.11, bf16[4,2,128,128]{3,2,1,0:T(8,128)(2,1)} %bitcast.12, ...), custom_call_target="tpu_custom_call" | custom-call | tf_op jit(solution)/shard_map/environments/pallas_call | solution.py:487
  117.0 0.0 copy-start
  117.0 1.7 %copy.14 = bf16[1,4,2,128,128]{4,3,2,1,0:T(8,128)(2,1)} copy(bf16[1,4,2,128,128]{4,3,2,1,0:T(8,128)(2,1)} %bitcast.15) | data formatting | bytes 524288
  118.8 0.0 copy-done
  118.8 0.7 copy.15
Async XLA Ops:
  1.3 0.7 copy-start.1
  117.0 1.7 %copy-start = (bf16[4,2,128,128]{3,2,1,0:T(8,128)(2,1)S(1)}, bf16[4,2,128,128]{3,2,1,0:T(8,128)(2,1)}, u32[]{:S(2)}) copy-start(bf16[4,2,128,128]{3,2,1,0:T(8,128)(2,1)} %get-tuple-element.5) | copy-start | bytes 786436

commit v5 on v4

--- a/solution.py
+++ b/solution.py
@@ -18,9 +18,9 @@
     sites, secs, steps,
     tab, energy, bond_add, canon_l, canon_r, seed_l, seed_r, site_in, bond_in,
     left_out, right_out,
-    own_c, own_s, tall, wab, hold, fresh, pbuf, give_n, got_n, give_r, got_r, give_c, lefts, nxt, rgt, site_v, bond_v,
+    own_c, tall, wab, hold, fresh, pbuf, give_n, got_n, give_r, got_r, give_c, lefts, nxt, rgt, site_v, bond_v,
     outer, gram_s, gram_r, unit_s, unit_r, fac_s, fac,
-    loc_sem, gsend, grecv, ssend, srecv, tsend, trecv, xsend, xrecv,
+    loc_sem, gsend, grecv, tsend, trecv, xsend, xrecv,
     usem, osend, orecv, fsend, frecv, psend, rsend, rrecv,
 ):
     site, sec = lax.axis_index("site"), lax.axis_index("sec")
@@ -42,8 +42,8 @@
     last = steps - 1
 
     loads = [
-        pltpu.make_async_copy(canon_l, own_c.at[0], loc_sem.at[0]),
-        pltpu.make_async_copy(canon_r, own_c.at[1], loc_sem.at[1]),
+        pltpu.make_async_copy(canon_l, own_c.at[0, pl.ds(1, phys)], loc_sem.at[0]),
+        pltpu.make_async_copy(canon_r, own_c.at[1, pl.ds(1, phys)], loc_sem.at[1]),
     ]
     center = [
         pltpu.make_async_copy(site_in, site_v, loc_sem.at[2]),
@@ -52,8 +52,8 @@
     for load in loads + center:
         load.start()
     for i in range(owned):
-        own_s[0, i] = seed_l[i]
-        own_s[1, i] = seed_r[i].T
+        own_c[0, 0, i] = seed_l[i]
+        own_c[1, 0, i] = seed_r[i].T
 
     barrier = pltpu.get_barrier_semaphore()
     others = [(dy, e) for dy in range(rows) for e in range(2) if (dy, e) != (0, 0)]
@@ -71,39 +71,61 @@
     pl.semaphore_wait(barrier, len(others) + 3)
 
     place = pl.ds(sec * owned, owned)
+    peer_place = pl.ds(peer_sec * owned, owned)
+    parts = (pl.ds(0, 3), pl.ds(3, phys - 2))
+    up_row, down_row = lax.rem(row + 1, rows), lax.rem(row + rows - 1, rows)
+    up, down = up_row * 2 + role, down_row * 2 + role
     sent = []
-    for n, (dy, e) in enumerate(others):
-        to, to_role = sec_of(dy, e)
-        sent.append(pltpu.make_async_remote_copy(
-            src_ref=own_s.at[to_role], dst_ref=hold.at[0, place],
-            send_sem=ssend.at[n], recv_sem=srecv.at[n],
-            device_id=(site, to), device_id_type=MESH))
+
+    def gather_copy(n, src, part, at, to, slot):
+        return pltpu.make_async_remote_copy(
+            src_ref=src, dst_ref=tall.at[part, at], send_sem=gsend.at[n], recv_sem=grecv.at[slot],
+            device_id=(site, to), device_id_type=MESH)
+
+    def give_on(src, part, at, to, slot):
+        sent.append(gather_copy(len(sent), src, part, at, to, slot))
         sent[-1].start()
+
+    def landed(part, at, slot):
+        gather_copy(0, tall.at[part, at], part, at, up, slot).wait_recv()
+
     for load in loads:
         load.wait()
-    keep = [
-        pltpu.make_async_copy(own_c.at[role], tall.at[:, place], loc_sem.at[0]),
-        pltpu.make_async_copy(own_s.at[role], hold.at[0, place], loc_sem.at[1]),
-    ]
-    for n, (dy, e) in enumerate(others):
-        to, to_role = sec_of(dy, e)
-        sent.append(pltpu.make_async_remote_copy(
-            src_ref=own_c.at[to_role], dst_ref=tall.at[:, place],
-            send_sem=gsend.at[n], recv_sem=grecv.at[n],
-            device_id=(site, to), device_id_type=MESH))
-        sent[-1].start()
-    for copy in keep:
-        copy.start()
-    for copy in keep:
-        copy.wait()
-    for copy in sent:
-        copy.wait_recv()
+    for h in range(2):
+        give_on(own_c.at[1 - role, parts[h]], parts[h], place, peer_sec, h)
+    for h in range(2):
+        give_on(own_c.at[role, parts[h]], parts[h], place, up, 2 + h)
+        give_on(own_c.at[role, parts[1 - h]], parts[1 - h], place, down, 9 - h)
+    keep = pltpu.make_async_copy(own_c.at[role], tall.at[:, place], loc_sem.at[0])
+    keep.start()
+
+    def block_at(of_row, of_peer):
+        return pl.ds((of_row * 2 + (1 - role if of_peer else role)) * owned, owned)
+
+    for h in range(2):
+        landed(parts[h], peer_place, h)
+        give_on(tall.at[parts[h], peer_place], parts[h], peer_place, up, 4 + h)
+        give_on(tall.at[parts[h], peer_place], parts[h], peer_place, down, 10 + h)
+        at = block_at(down_row, h)
+        landed(parts[0], at, 2 + 2 * h)
+        give_on(tall.at[parts[0], at], parts[0], at, up, 6 + h)
+        at = block_at(up_row, h)
+        landed(parts[1], at, 9 + 2 * h)
+        give_on(tall.at[parts[1], at], parts[1], at, down, 12 + h)
+    keep.wait()
+    far_row = lax.rem(row + 2, rows)
+    for h in range(2):
+        landed(parts[1], block_at(down_row, h), 3 + 2 * h)
+        landed(parts[0], block_at(up_row, h), 8 + 2 * h)
+        landed(parts[0], block_at(far_row, h), 6 + h)
+        landed(parts[1], block_at(far_row, h), 12 + h)
 
     def arrange(i, carry):
+        hold[0, i] = tall[0, i]
         for s in range(phys):
             cols = slice(s * width, (s + 1) * width)
-            wab[role, i, :, cols] = tall[s, tab[1, s, i]]
-            wab[1 - role, i, :, cols] = tall[s, i].T
+            wab[role, i, :, cols] = tall[1 + s, tab[1, s, i]]
+            wab[1 - role, i, :, cols] = tall[1 + s, i].T
         return carry
 
     lax.fori_loop(0, sectors, arrange, 0)
@@ -493,9 +515,8 @@
         in_specs=[smem, smem, smem, hbm, hbm, vmem, vmem, hbm, hbm],
         out_specs=(vmem, vmem),
         scratch_shapes=[
-            pltpu.VMEM((2, phys, owned, *block), bf16),
-            pltpu.VMEM((2, owned, *block), bf16),
-            pltpu.VMEM((phys, sectors, *block), bf16),
+            pltpu.VMEM((2, 1 + phys, owned, *block), bf16),
+            pltpu.VMEM((1 + phys, sectors, *block), bf16),
             pltpu.VMEM((2, sectors, width, phys * width), bf16),
             pltpu.VMEM((steps + 1, sectors, *block), bf16),
             pltpu.VMEM((steps, sectors, *block), bf16),
@@ -516,7 +537,7 @@
             pltpu.VMEM((owned, *block), f32),
             pltpu.VMEM((owned, *block), bf16),
             pltpu.VMEM((sectors, *block), bf16),
-            dma((4,)), dma((secs - 1,)), dma((secs - 1,)), dma((secs - 1,)), dma((secs - 1,)),
+            dma((4,)), dma((14,)), dma((14,)),
             dma((steps, 4)), dma((steps, 4)), dma((2,)), dma((2,)),
             dma((2,)), dma((secs,)), dma((secs,)), dma((secs - 1,)), dma((secs - 1,)),
             dma((steps,)), dma((2,)), dma((1,)),

time: 121 us -> 114 us (0.942); the launches traced: 119 us -> 114 us
  Pallas kernels: 114 us -> 109 us
    pallas_call x1, Pallas kernels: 114 us -> 109 us  [update(): pl.pallas_call(functools.partial(update_kernel, sites, secs, steps), out_...]
where the time goes in v5:
time: 114 us
  Pallas kernels  109 us (96%)
  local copies, waits for them, and re-layouts  3.09 us (3%)
  between operations  1.3 us (1%)
    pallas_call x1, Pallas kernels, update(): pl.pallas_call(functools.partial(update_kernel, sites, secs, steps), out_...  109 us
    unnamed x6, local copies, waits for them, and re-layouts  3.09 us

profile of v5, /device:TPU:2, one launch (start us, length us, event | category | flops | bytes accessed | tf_op | source)
XLA Modules:
  0.0 113.8 jit_solution(14175507164245340395)
XLA Ops:
  1.3 0.0 copy-start.1
  1.3 0.7 copy-done.1
  2.0 0.1 select_reduce_fusion
  2.1 0.6 pad_add_fusion.tab
  2.7 108.7 %environments.1 = (bf16[4,2,128,128]{3,2,1,0:T(8,128)(2,1)}, bf16[4,2,128,128]{3,2,1,0:T(8,128)(2,1)}) custom-call(s32[2,4,16]{2,1,0:T(4,128)} %pad_add_fusion.tab, f32[4]{0:T(128)} %bitcast.21, f32[1]{0:T(128)S(6)} %copy.13.bond_add, bf16[4,2,128,128]{3,2,1,0:T(8,128)(2,1)} %bitcast.11, bf16[4,2,128,128]{3,2,1,0:T(8,128)(2,1)} %bitcast.12, ...), custom_call_target="tpu_custom_call" | custom-call | tf_op jit(solution)/shard_map/environments/pallas_call | solution.py:509
  111.3 0.0 copy-start
  111.4 1.7 %copy.14 = bf16[1,4,2,128,128]{4,3,2,1,0:T(8,128)(2,1)} copy(bf16[1,4,2,128,128]{4,3,2,1,0:T(8,128)(2,1)} %bitcast.15) | data formatting | bytes 524288
  113.1 0.0 copy-done
  113.1 0.7 copy.15
Async XLA Ops:
  1.3 0.7 copy-start.1
  111.3 1.7 %copy-start = (bf16[4,2,128,128]{3,2,1,0:T(8,128)(2,1)S(1)}, bf16[4,2,128,128]{3,2,1,0:T(8,128)(2,1)}, u32[]{:S(2)}) copy-start(bf16[4,2,128,128]{3,2,1,0:T(8,128)(2,1)} %get-tuple-element.5) | copy-start | bytes 786436

commit v6 on v5

--- a/solution.py
+++ b/solution.py
@@ -16,12 +16,12 @@
 
 def update_kernel(
     sites, secs, steps,
-    tab, energy, bond_add, canon_l, canon_r, seed_l, seed_r, site_in, bond_in,
+    tab, own_tab, energy, bond_add, canon_l, canon_r, seed_l, seed_r, site_in, bond_in,
     left_out, right_out,
-    own_c, tall, wab, hold, fresh, pbuf, give_n, got_n, give_r, got_r, give_c, lefts, nxt, rgt, site_v, bond_v,
+    own_c, tall, wab, hold, fresh, pbuf, give_n, got_n, give_r, got_r, give_c, lefts, tab_v, tab_n, nxt, rgt, site_v, bond_v,
     outer, gram_s, gram_r, unit_s, unit_r, fac_s, fac,
     loc_sem, gsend, grecv, tsend, trecv, xsend, xrecv,
-    usem, osend, orecv, fsend, frecv, psend, rsend, rrecv,
+    usem, osend, orecv, fsend, frecv, psend, rsend, rrecv, bsem, lsend, lrecv,
 ):
     site, sec = lax.axis_index("site"), lax.axis_index("sec")
     role = lax.rem(sec, 2)
@@ -45,15 +45,16 @@
         pltpu.make_async_copy(canon_l, own_c.at[0, pl.ds(1, phys)], loc_sem.at[0]),
         pltpu.make_async_copy(canon_r, own_c.at[1, pl.ds(1, phys)], loc_sem.at[1]),
     ]
+    seeds = [
+        pltpu.make_async_copy(seed_l, own_c.at[0, 0], loc_sem.at[4]),
+        pltpu.make_async_copy(seed_r, own_c.at[1, 0], loc_sem.at[5]),
+    ]
     center = [
         pltpu.make_async_copy(site_in, site_v, loc_sem.at[2]),
         pltpu.make_async_copy(bond_in, bond_v, loc_sem.at[3]),
     ]
-    for load in loads + center:
+    for load in seeds + loads + center:
         load.start()
-    for i in range(owned):
-        own_c[0, 0, i] = seed_l[i]
-        own_c[1, 0, i] = seed_r[i].T
 
     barrier = pltpu.get_barrier_semaphore()
     others = [(dy, e) for dy in range(rows) for e in range(2) if (dy, e) != (0, 0)]
@@ -68,6 +69,10 @@
         pl.semaphore_signal(barrier, inc=1, device_id=(other, sec), device_id_type=MESH)
     across = lax.rem(site + 1 - 2 * role + sites, sites)
     pl.semaphore_signal(barrier, inc=1, device_id=(across, peer_sec), device_id_type=MESH)
+    for load in seeds:
+        load.wait()
+    for i in range(owned):
+        own_c[1, 0, i] = own_c[1, 0, i].T
     pl.semaphore_wait(barrier, len(others) + 3)
 
     place = pl.ds(sec * owned, owned)
@@ -89,6 +94,10 @@
     def landed(part, at, slot):
         gather_copy(0, tall.at[part, at], part, at, up, slot).wait_recv()
 
+    tab_copy = pltpu.make_async_remote_copy(
+        src_ref=own_tab, dst_ref=tab_v, send_sem=bsem.at[0], recv_sem=bsem.at[1],
+        device_id=(source, sec), device_id_type=MESH)
+    tab_copy.start()
     for load in loads:
         load.wait()
     for h in range(2):
@@ -113,22 +122,41 @@
         landed(parts[1], at, 9 + 2 * h)
         give_on(tall.at[parts[1], at], parts[1], at, down, 12 + h)
     keep.wait()
+
+    def turned(start, count):
+        def body(n, carry):
+            i = start + n
+            hold[0, i] = tall[0, i]
+            for s in range(phys):
+                wab[1 - role, i, :, s * width : (s + 1) * width] = tall[1 + s, i].T
+            return carry
+
+        lax.fori_loop(0, count, body, 0)
+
+    def row_at(of_row):
+        return of_row * 2 * owned
+
+    turned(row_at(row), 2 * owned)
+    for h in range(2):
+        landed(parts[1], block_at(down_row, h), 3 + 2 * h)
+    turned(row_at(down_row), 2 * owned)
+    for h in range(2):
+        landed(parts[0], block_at(up_row, h), 8 + 2 * h)
+    turned(row_at(up_row), 2 * owned)
     far_row = lax.rem(row + 2, rows)
     for h in range(2):
-        landed(parts[1], block_at(down_row, h), 3 + 2 * h)
-        landed(parts[0], block_at(up_row, h), 8 + 2 * h)
         landed(parts[0], block_at(far_row, h), 6 + h)
         landed(parts[1], block_at(far_row, h), 12 + h)
-
-    def arrange(i, carry):
-        hold[0, i] = tall[0, i]
+    turned(row_at(far_row), 2 * owned)
+    tab_copy.wait_recv()
+    pltpu.sync_copy(tab_v, tab_n)
+
+    def in_order(i, carry):
         for s in range(phys):
-            cols = slice(s * width, (s + 1) * width)
-            wab[role, i, :, cols] = tall[1 + s, tab[1, s, i]]
-            wab[1 - role, i, :, cols] = tall[1 + s, i].T
+            wab[role, i, :, s * width : (s + 1) * width] = tall[1 + s, tab[1, s, i]]
         return carry
 
-    lax.fori_loop(0, sectors, arrange, 0)
+    lax.fori_loop(0, sectors, in_order, 0)
 
     def to_target(t, c, part):
         return pltpu.make_async_remote_copy(
@@ -194,28 +222,25 @@
         def _():
             for c in range(3):
                 apply_left(t, far_at[c], FAR[c])
-                send(far_copy(t, c))
+                if send:
+                    far_copy(t, c).start()
             apply_left(t, far_at[3], FAR[3])
 
         @pl.when(jnp.logical_not(far_target))
         def _():
             for c in range(len(NEAR)):
                 apply_left(t, near_at[c], NEAR[c])
-                send(near_copy(t, c))
-
-    def send_left(copy):
-        @pl.when(role == 0)
-        def _():
-            copy.start()
+                if send:
+                    near_copy(t, c).start()
 
     def turn(t, carry):
         first_half(t)
-        second_half(t, lambda copy: copy.start())
+        second_half(t, True)
         return carry
 
     lax.fori_loop(0, last, turn, 0)
     first_half(last)
-    second_half(last, send_left)
+    second_half(last, False)
     for load in center:
         load.wait()
 
@@ -235,12 +260,15 @@
     def scaled(block, scale):
         return (block.astype(f32) * scale).astype(bf16)
 
-    cur_copy = pltpu.make_async_remote_copy(
-        src_ref=give_c, dst_ref=lefts, send_sem=xsend.at[0], recv_sem=xrecv.at[0],
-        device_id=(site, peer_sec), device_id_type=MESH)
+    def left_copy(n, i):
+        return pltpu.make_async_remote_copy(
+            src_ref=give_c.at[n, i], dst_ref=lefts.at[i],
+            send_sem=lsend.at[n, i], recv_sem=lrecv.at[i],
+            device_id=(target, (peer_sec, sec)[n]), device_id_type=MESH)
+
     nxt_copy = pltpu.make_async_remote_copy(
         src_ref=give_n, dst_ref=got_n,
-        send_sem=xsend.at[1], recv_sem=xrecv.at[1],
+        send_sem=xsend.at[0], recv_sem=xrecv.at[0],
         device_id=(site, peer_sec), device_id_type=MESH)
     rgt_copies = [pltpu.make_async_remote_copy(
         src_ref=give_r.at[n], dst_ref=got_r,
@@ -251,31 +279,13 @@
     def _():
         scale_next = scale_of(fresh, last)
         for i in range(owned):
+            for n, start in enumerate((peer_at, own_at)):
+                for s in range(phys):
+                    give_c[n, i, s] = scaled(fresh[last, tab_n[s, start + i]], scale_next)
+                left_copy(n, i).start()
             give_n[i] = scaled(fresh[last, peer_at + i], scale_next)
+            nxt[i] = scaled(fresh[last, own_at + i], scale_next)
         nxt_copy.start()
-        for i in range(owned):
-            nxt[i] = scaled(fresh[last, own_at + i], scale_next)
-
-        @pl.when(far_source)
-        def _():
-            for c in range(4):
-                far_copy(last, c).wait_recv()
-                if c == 0:
-                    pair_copy(last).start()
-
-        @pl.when(jnp.logical_not(far_source))
-        def _():
-            for c in range(len(NEAR)):
-                near_copy(last, c).wait_recv()
-
-        scale_cur = scale_of(hold, steps)
-        for i in range(owned):
-            for s in range(phys):
-                give_c[s, i] = scaled(hold[steps, tab[0, s, peer_at + i]], scale_cur)
-        cur_copy.start()
-        for i in range(owned):
-            for s in range(phys):
-                lefts[s, i] = scaled(hold[steps, tab[0, s, own_at + i]], scale_cur)
 
     @pl.when(role == 1)
     def _():
@@ -284,9 +294,6 @@
             for i in range(owned):
                 give_r[n, i] = scaled(fresh[last, start + i], scale_right)
             rgt_copies[n].start()
-        nxt_copy.wait_recv()
-        for i in range(owned):
-            nxt[i] = got_n[i]
 
     rgt_copies[0].wait_recv()
     for i in range(owned):
@@ -341,36 +348,13 @@
     def with_itself(x, dim):
         return lax.dot_general(x, x, (((dim,), (dim,)), ((), ())), preferred_element_type=f32)
 
-    grams = []
-    for i in range(owned):
-        bond = bond_v[i]
-        for repeat in range(NAPP):
-            half = jnp.dot(nxt[i], bond, preferred_element_type=f32).astype(bf16)
-            bond = (
-                jnp.dot(half, rgt[i], preferred_element_type=f32) + bond_add[0] * bond.astype(f32)
-            ).astype(bf16)
-        bond_v[i] = bond
-        grams.append(with_itself(bond, 0))
-    for i, root in enumerate(inverse_roots(grams)):
-        turned = bond_v[i].T
-        unit_s[i] = jnp.dot(
-            as_lhs(split(root)), jnp.concatenate([turned, turned], axis=0), preferred_element_type=f32
-        )
-    unit_copy = pltpu.make_async_remote_copy(
-        src_ref=unit_s, dst_ref=unit_r, send_sem=usem.at[0], recv_sem=usem.at[1],
-        device_id=(lax.rem(site + 1, sites), sec), device_id_type=MESH)
-    unit_copy.start()
-
-    @pl.when(role == 1)
-    def _():
-        cur_copy.wait_recv()
-
-    for i in range(owned):
+    for i in range(owned):
+        left_copy(0, i).wait_recv()
         nows = [site_v[s, i] for s in range(phys)]
         for repeat in range(NAPP):
             halves = jnp.concatenate(
                 [
-                    jnp.dot(lefts[s, i], nows[s], preferred_element_type=f32).astype(bf16)
+                    jnp.dot(lefts[i, s], nows[s], preferred_element_type=f32).astype(bf16)
                     for s in range(phys)
                 ],
                 axis=0,
@@ -412,8 +396,39 @@
 
     lax.fori_loop(0, secs, pack, 0)
 
-    stacks = [jnp.concatenate([site_v[s, i] for s in range(phys)], axis=0) for i in range(owned)]
-    roots = inverse_roots([with_itself(stack, 0) for stack in stacks])
+    @pl.when(role == 1)
+    def _():
+        nxt_copy.wait_recv()
+        for i in range(owned):
+            nxt[i] = got_n[i]
+
+    for i in range(owned):
+        bond = bond_v[i]
+        for repeat in range(NAPP):
+            half_bond = jnp.dot(nxt[i], bond, preferred_element_type=f32).astype(bf16)
+            bond = (
+                jnp.dot(half_bond, rgt[i], preferred_element_type=f32)
+                + bond_add[0] * bond.astype(f32)
+            ).astype(bf16)
+        bond_v[i] = bond
+
+    grams = [with_itself(bond_v[i], 0) for i in range(owned)]
+    for i in range(owned):
+        stack = jnp.concatenate([site_v[s, i] for s in range(phys)], axis=0)
+        grams.append(with_itself(stack, 0))
+    roots = inverse_roots(grams)
+    for i in range(owned):
+        turned_bond = bond_v[i].T
+        unit_s[i] = jnp.dot(
+            as_lhs(split(roots[i])),
+            jnp.concatenate([turned_bond, turned_bond], axis=0),
+            preferred_element_type=f32,
+        )
+    unit_copy = pltpu.make_async_remote_copy(
+        src_ref=unit_s, dst_ref=unit_r, send_sem=usem.at[0], recv_sem=usem.at[1],
+        device_id=(lax.rem(site + 1, sites), sec), device_id_type=MESH)
+    unit_copy.start()
+    roots = roots[owned:]
     for i in range(owned):
         factor = product(as_lhs(split(roots[i])), as_rhs(split(unit_s[i]))).astype(bf16)
         stack = jnp.concatenate([site_v[s, i] for s in range(phys)], axis=0)
@@ -458,7 +473,7 @@
                 fac[tab[0, s, own_at + i]], site_v[s, i], preferred_element_type=f32
             ).astype(bf16)
 
-    for copy in sent + fac_copies + [unit_copy]:
+    for copy in sent + fac_copies + [unit_copy, tab_copy]:
         copy.wait_send()
     for n in range(secs - 1):
         gram_copy(lax.rem(sec + 1 + n, secs)).wait_send()
@@ -484,9 +499,10 @@
 
     @pl.when(role == 0)
     def _():
-        drain(last, 0)
         nxt_copy.wait_send()
-        cur_copy.wait_send()
+        for i in range(owned):
+            for n in range(2):
+                left_copy(n, i).wait_send()
 
     @pl.when(role == 1)
     def _():
@@ -494,7 +510,7 @@
             copy.wait_send()
 
 
-def update(tables, energy, bond_add, canon_l, canon_r, seed_l, seed_r, site, bond):
+def update(tables, own_table, energy, bond_add, canon_l, canon_r, seed_l, seed_r, site, bond):
     sites, secs = lax.axis_size("site"), lax.axis_size("sec")
     steps = sites // 4
     phys, owned, width = canon_l.shape[:3]
@@ -504,7 +520,7 @@
     dma = pltpu.SemaphoreType.DMA
     smem = pl.BlockSpec(memory_space=pltpu.SMEM)
     vmem = pl.BlockSpec(memory_space=pltpu.VMEM)
-    hbm = pl.BlockSpec(memory_space=pl.ANY)
+    hbm = pl.BlockSpec(memory_space=pltpu.HBM)
     mail = pltpu.VMEM((secs, width + 8, width), f32)
     return pl.pallas_call(
         functools.partial(update_kernel, sites, secs, steps),
@@ -512,21 +528,23 @@
             jax.ShapeDtypeStruct((phys, owned, *block), bf16),
             jax.ShapeDtypeStruct((phys, owned, *block), bf16),
         ),
-        in_specs=[smem, smem, smem, hbm, hbm, vmem, vmem, hbm, hbm],
+        in_specs=[smem, vmem, smem, smem] + [hbm] * 6,
         out_specs=(vmem, vmem),
         scratch_shapes=[
             pltpu.VMEM((2, 1 + phys, owned, *block), bf16),
             pltpu.VMEM((1 + phys, sectors, *block), bf16),
             pltpu.VMEM((2, sectors, width, phys * width), bf16),
-            pltpu.VMEM((steps + 1, sectors, *block), bf16),
+            pltpu.VMEM((steps, sectors, *block), bf16),
             pltpu.VMEM((steps, sectors, *block), bf16),
             pltpu.VMEM((sectors, phys, *block), bf16),
             pltpu.VMEM((owned, *block), bf16),
             pltpu.VMEM((owned, *block), bf16),
             pltpu.VMEM((2, owned, *block), bf16),
             pltpu.VMEM((owned, *block), bf16),
-            pltpu.VMEM((phys, owned, *block), bf16),
-            pltpu.VMEM((phys, owned, *block), bf16),
+            pltpu.VMEM((2, owned, phys, *block), bf16),
+            pltpu.VMEM((owned, phys, *block), bf16),
+            pltpu.VMEM((8, 128), jnp.int32),
+            pltpu.SMEM((8, 128), jnp.int32),
             pltpu.VMEM((owned, *block), bf16),
             pltpu.VMEM((owned, *block), bf16),
             pltpu.VMEM((phys, owned, *block), bf16),
@@ -537,16 +555,23 @@
             pltpu.VMEM((owned, *block), f32),
             pltpu.VMEM((owned, *block), bf16),
             pltpu.VMEM((sectors, *block), bf16),
-            dma((4,)), dma((14,)), dma((14,)),
-            dma((steps, 4)), dma((steps, 4)), dma((2,)), dma((2,)),
+            dma((6,)), dma((14,)), dma((14,)),
+            dma((steps, 4)), dma((steps, 4)), dma((1,)), dma((1,)),
             dma((2,)), dma((secs,)), dma((secs,)), dma((secs - 1,)), dma((secs - 1,)),
             dma((steps,)), dma((2,)), dma((1,)),
+            dma((2,)), dma((2, owned)), dma((owned,)),
         ],
         compiler_params=pltpu.CompilerParams(
-            collective_id=0, has_side_effects=True, vmem_limit_bytes=56 * 1024 * 1024
+            collective_id=0, has_side_effects=True, vmem_limit_bytes=30 * 1024 * 1024
         ),
         name="environments",
-    )(tables, energy, bond_add, canon_l, canon_r, seed_l, seed_r, site, bond)
+    )(
+        tables, own_table, energy, bond_add,
+        *(
+            pltpu.with_memory_space_constraint(x, pltpu.HBM)
+            for x in (canon_l, canon_r, seed_l, seed_r, site, bond)
+        ),
+    )
 
 
 def per_device(
@@ -565,8 +590,10 @@
     right_of = jnp.sum(
         jnp.where(sources[:, :, None] == labels[None, None, :], labels[None, :, None], 0), axis=1
     )
+    phys, sectors = sources.shape
+    own_table = jnp.pad(sources, ((0, 8 - phys), (0, 128 - sectors)))
     left_new, right_new = update(
-        jnp.stack([sources, right_of]), onsite[0], bond_shift, left_canon[0], right_canon[0],
+        jnp.stack([sources, right_of]), own_table, onsite[0], bond_shift, left_canon[0], right_canon[0],
         left_seed[0], right_seed[0], center_site[0], center_bond[0],
     )
     return (left_new[None], right_new[None])

time: 114 us -> 111 us (0.974)
  Pallas kernels: 109 us -> 106 us
    pallas_call x1, Pallas kernels: 109 us -> 106 us  [update(): pl.pallas_call(functools.partial(update_kernel, sites, secs, steps), out_...]
where the time goes in v6:
time: 111 us; the launch traced here: 110 us
  Pallas kernels  106 us (95%)
  local copies, waits for them, and re-layouts  2.73 us (2%)
  between operations  1.31 us (1%)
    pallas_call x1, Pallas kernels, update(): pl.pallas_call(functools.partial(update_kernel, sites, secs, steps), out_...  106 us
    unnamed x6, local copies, waits for them, and re-layouts  2.72 us

profile of v6, /device:TPU:2, one launch (start us, length us, event | category | flops | bytes accessed | tf_op | source)
XLA Modules:
  0.0 109.8 jit_solution(10786150034067753510)
XLA Ops:
  1.3 0.0 copy-start.1
  1.3 0.7 copy-done.1
  2.0 0.1 select_reduce_fusion
  2.1 0.0 copy-start
  2.1 0.6 copy-done
  2.7 105.7 %environments.1 = (bf16[4,2,128,128]{3,2,1,0:T(8,128)(2,1)S(1)}, bf16[4,2,128,128]{3,2,1,0:T(8,128)(2,1)S(1)}) custom-call(s32[2,4,16]{2,1,0:T(4,128)S(1)} %pad_add_fusion.tab, s32[8,128]{1,0:T(8,128)S(1)} %pad.4.own_tab, f32[4]{0:T(128)S(1)} %bitcast.13, f32[1]{0:T(128)S(6)} %copy.13.bond_add, bf16[4,2,128,128]{3,2,1,0:T(8,128)(2,1)} %bitcast.14, ...), custom_call_target="tpu_custom_call" | custom-call | tf_op jit(solution)/shard_map/environments/pallas_call | solution.py:525
  108.4 0.7 copy.14
  109.1 0.7 copy.15
  (2 shorter events, 0.0 us)
Async XLA Ops:
  1.3 0.7 copy-start.1
  2.1 0.7 copy-start

commit v7 on v6

--- a/solution.py
+++ b/solution.py
@@ -16,9 +16,9 @@
 
 def update_kernel(
     sites, secs, steps,
-    tab, own_tab, energy, bond_add, canon_l, canon_r, seed_l, seed_r, site_in, bond_in,
+    src_tab, own_tab, energy_in, bond_add, canon_l, canon_r, seed_l, seed_r, site_in, bond_in,
     left_out, right_out,
-    own_c, tall, wab, hold, fresh, pbuf, give_n, got_n, give_r, got_r, give_c, lefts, tab_v, tab_n, nxt, rgt, site_v, bond_v,
+    own_c, tall, wab, hold, fresh, pbuf, give_n, got_n, give_r, got_r, give_c, lefts, tab, tab_v, tab_n, energy, nxt, rgt, site_v, bond_v,
     outer, gram_s, gram_r, unit_s, unit_r, fac_s, fac,
     loc_sem, gsend, grecv, tsend, trecv, xsend, xrecv,
     usem, osend, orecv, fsend, frecv, psend, rsend, rrecv, bsem, lsend, lrecv,
@@ -52,6 +52,7 @@
     center = [
         pltpu.make_async_copy(site_in, site_v, loc_sem.at[2]),
         pltpu.make_async_copy(bond_in, bond_v, loc_sem.at[3]),
+        pltpu.make_async_copy(energy_in, energy, loc_sem.at[6]),
     ]
     for load in seeds + loads + center:
         load.start()
@@ -122,6 +123,17 @@
         landed(parts[1], at, 9 + 2 * h)
         give_on(tall.at[parts[1], at], parts[1], at, down, 12 + h)
     keep.wait()
+
+    def tabulate(n, carry):
+        s, m = n // sectors, lax.rem(n, sectors)
+        joined = jnp.int32(0)
+        for k in range(sectors):
+            joined = jnp.where(src_tab[s, k] == m, k, joined)
+        tab[0, s, m] = src_tab[s, m]
+        tab[1, s, m] = joined
+        return carry
+
+    lax.fori_loop(0, phys * sectors, tabulate, 0)
 
     def turned(start, count):
         def body(n, carry):
@@ -361,7 +373,7 @@
             )
             done = jnp.dot(halves, rgt[i], preferred_element_type=f32)
             nows = [
-                (done[s * width : (s + 1) * width] + energy[s] * nows[s].astype(f32)).astype(bf16)
+                (done[s * width : (s + 1) * width] + energy[0, s] * nows[s].astype(f32)).astype(bf16)
                 for s in range(phys)
             ]
         for s in range(phys):
@@ -412,11 +424,7 @@
             ).astype(bf16)
         bond_v[i] = bond
 
-    grams = [with_itself(bond_v[i], 0) for i in range(owned)]
-    for i in range(owned):
-        stack = jnp.concatenate([site_v[s, i] for s in range(phys)], axis=0)
-        grams.append(with_itself(stack, 0))
-    roots = inverse_roots(grams)
+    roots = inverse_roots([with_itself(bond_v[i], 0) for i in range(owned)])
     for i in range(owned):
         turned_bond = bond_v[i].T
         unit_s[i] = jnp.dot(
@@ -428,14 +436,6 @@
         src_ref=unit_s, dst_ref=unit_r, send_sem=usem.at[0], recv_sem=usem.at[1],
         device_id=(lax.rem(site + 1, sites), sec), device_id_type=MESH)
     unit_copy.start()
-    roots = roots[owned:]
-    for i in range(owned):
-        factor = product(as_lhs(split(roots[i])), as_rhs(split(unit_s[i]))).astype(bf16)
-        stack = jnp.concatenate([site_v[s, i] for s in range(phys)], axis=0)
-        fresh_left = jnp.dot(stack, factor, preferred_element_type=f32).astype(bf16)
-        for s in range(phys):
-            left_out[s, i] = fresh_left[s * width : (s + 1) * width]
-
     def gram_from(d):
         return pltpu.make_async_remote_copy(
             src_ref=gram_s.at[d], dst_ref=gram_r.at[d], send_sem=osend.at[d], recv_sem=orecv.at[d],
@@ -465,6 +465,19 @@
         fac_copies[-1].start()
     for i in range(owned):
         fac[own_at + i] = fac_s[i]
+
+    grams = []
+    for i in range(owned):
+        stack = jnp.concatenate([site_v[s, i] for s in range(phys)], axis=0)
+        grams.append(with_itself(stack, 0))
+    roots = inverse_roots(grams)
+    for i in range(owned):
+        factor = product(as_lhs(split(roots[i])), as_rhs(split(unit_s[i]))).astype(bf16)
+        stack = jnp.concatenate([site_v[s, i] for s in range(phys)], axis=0)
+        fresh_left = jnp.dot(stack, factor, preferred_element_type=f32).astype(bf16)
+        for s in range(phys):
+            left_out[s, i] = fresh_left[s * width : (s + 1) * width]
+
     for copy in fac_copies:
         copy.wait_recv()
     for i in range(owned):
@@ -510,7 +523,7 @@
             copy.wait_send()
 
 
-def update(tables, own_table, energy, bond_add, canon_l, canon_r, seed_l, seed_r, site, bond):
+def update(table, energy, bond_add, canon_l, canon_r, seed_l, seed_r, site, bond):
     sites, secs = lax.axis_size("site"), lax.axis_size("sec")
     steps = sites // 4
     phys, owned, width = canon_l.shape[:3]
@@ -528,7 +541,7 @@
             jax.ShapeDtypeStruct((phys, owned, *block), bf16),
             jax.ShapeDtypeStruct((phys, owned, *block), bf16),
         ),
-        in_specs=[smem, vmem, smem, smem] + [hbm] * 6,
+        in_specs=[smem, hbm, hbm, smem] + [hbm] * 6,
         out_specs=(vmem, vmem),
         scratch_shapes=[
             pltpu.VMEM((2, 1 + phys, owned, *block), bf16),
@@ -543,8 +556,10 @@
             pltpu.VMEM((owned, *block), bf16),
             pltpu.VMEM((2, owned, phys, *block), bf16),
             pltpu.VMEM((owned, phys, *block), bf16),
-            pltpu.VMEM((8, 128), jnp.int32),
-            pltpu.SMEM((8, 128), jnp.int32),
+            pltpu.SMEM((2, phys, sectors), jnp.int32),
+            pltpu.VMEM((phys, sectors), jnp.int32),
+            pltpu.SMEM((phys, sectors), jnp.int32),
+            pltpu.SMEM((1, phys), f32),
             pltpu.VMEM((owned, *block), bf16),
             pltpu.VMEM((owned, *block), bf16),
             pltpu.VMEM((phys, owned, *block), bf16),
@@ -555,7 +570,7 @@
             pltpu.VMEM((owned, *block), f32),
             pltpu.VMEM((owned, *block), bf16),
             pltpu.VMEM((sectors, *block), bf16),
-            dma((6,)), dma((14,)), dma((14,)),
+            dma((7,)), dma((14,)), dma((14,)),
             dma((steps, 4)), dma((steps, 4)), dma((1,)), dma((1,)),
             dma((2,)), dma((secs,)), dma((secs,)), dma((secs - 1,)), dma((secs - 1,)),
             dma((steps,)), dma((2,)), dma((1,)),
@@ -566,7 +581,8 @@
         ),
         name="environments",
     )(
-        tables, own_table, energy, bond_add,
+        table, pltpu.with_memory_space_constraint(table, pltpu.HBM),
+        pltpu.with_memory_space_constraint(energy, pltpu.HBM), bond_add,
         *(
             pltpu.with_memory_space_constraint(x, pltpu.HBM)
             for x in (canon_l, canon_r, seed_l, seed_r, site, bond)
@@ -585,15 +601,8 @@
     onsite,
     bond_shift,
 ):
-    sources = left_sector[0]
-    labels = jnp.arange(sources.shape[1], dtype=jnp.int32)
-    right_of = jnp.sum(
-        jnp.where(sources[:, :, None] == labels[None, None, :], labels[None, :, None], 0), axis=1
-    )
-    phys, sectors = sources.shape
-    own_table = jnp.pad(sources, ((0, 8 - phys), (0, 128 - sectors)))
     left_new, right_new = update(
-        jnp.stack([sources, right_of]), own_table, onsite[0], bond_shift, left_canon[0], right_canon[0],
+        left_sector[0], onsite, bond_shift, left_canon[0], right_canon[0],
         left_seed[0], right_seed[0], center_site[0], center_bond[0],
     )
     return (left_new[None], right_new[None])

time: 111 us -> 108 us (0.973)
  local copies, waits for them, and re-layouts: 2.73 us -> 1.41 us
    unnamed x6 -> x2, local copies, waits for them, and re-layouts: 2.72 us -> 1.41 us
where the time goes in v7:
time: 108 us; the launch traced here: 107 us
  Pallas kernels  105 us (97%)
  local copies, waits for them, and re-layouts  1.41 us (1%)
  between operations  1.29 us (1%)
    pallas_call x1, Pallas kernels, update(): pl.pallas_call(functools.partial(update_kernel, sites, secs, steps), out_...  105 us

profile of v7, /device:TPU:2, one launch (start us, length us, event | category | flops | bytes accessed | tf_op | source)
XLA Modules:
  0.0 107.3 jit_solution(10714438164922578611)
XLA Ops:
  1.3 104.6 %environments.1 = (bf16[4,2,128,128]{3,2,1,0:T(8,128)(2,1)S(1)}, bf16[4,2,128,128]{3,2,1,0:T(8,128)(2,1)S(1)}) custom-call(s32[4,16]{1,0:T(4,128)} %bitcast.17, s32[4,16]{1,0:T(4,128)} %bitcast.18, f32[1,4]{1,0:T(1,128)} %energy_in.1, f32[1]{0:T(128)S(6)} %copy.13.bond_add, bf16[4,2,128,128]{3,2,1,0:T(8,128)(2,1)} %bitcast.11, ...), custom_call_target="tpu_custom_call" | custom-call | tf_op jit(solution)/shard_map/environments/pallas_call | solution.py:538
  105.9 0.7 copy.14
  106.6 0.7 copy.15

commit v8 on v7

--- a/solution.py
+++ b/solution.py
@@ -101,7 +101,7 @@
     tab_copy.start()
     for load in loads:
         load.wait()
-    for h in range(2):
+    for h in (1, 0):
         give_on(own_c.at[1 - role, parts[h]], parts[h], place, peer_sec, h)
     for h in range(2):
         give_on(own_c.at[role, parts[h]], parts[h], place, up, 2 + h)
@@ -113,15 +113,18 @@
         return pl.ds((of_row * 2 + (1 - role if of_peer else role)) * owned, owned)
 
     for h in range(2):
-        landed(parts[h], peer_place, h)
-        give_on(tall.at[parts[h], peer_place], parts[h], peer_place, up, 4 + h)
-        give_on(tall.at[parts[h], peer_place], parts[h], peer_place, down, 10 + h)
+        part = parts[1 - h]
+        landed(part, peer_place, 1 - h)
+        give_on(tall.at[part, peer_place], part, peer_place, up, 5 - h)
+        give_on(tall.at[part, peer_place], part, peer_place, down, 11 - h)
+        part = parts[h]
         at = block_at(down_row, h)
-        landed(parts[0], at, 2 + 2 * h)
-        give_on(tall.at[parts[0], at], parts[0], at, up, 6 + h)
+        landed(part, at, 2 + 3 * h)
+        give_on(tall.at[part, at], part, at, up, 6 + h)
+        part = parts[1 - h]
         at = block_at(up_row, h)
-        landed(parts[1], at, 9 + 2 * h)
-        give_on(tall.at[parts[1], at], parts[1], at, down, 12 + h)
+        landed(part, at, 9 + h)
+        give_on(tall.at[part, at], part, at, down, 12 + h)
     keep.wait()
 
     def tabulate(n, carry):
@@ -150,15 +153,15 @@
 
     turned(row_at(row), 2 * owned)
     for h in range(2):
-        landed(parts[1], block_at(down_row, h), 3 + 2 * h)
+        landed(parts[1 - h], block_at(down_row, h), 3 + h)
     turned(row_at(down_row), 2 * owned)
     for h in range(2):
-        landed(parts[0], block_at(up_row, h), 8 + 2 * h)
+        landed(parts[h], block_at(up_row, h), 8 + 3 * h)
     turned(row_at(up_row), 2 * owned)
     far_row = lax.rem(row + 2, rows)
     for h in range(2):
-        landed(parts[0], block_at(far_row, h), 6 + h)
-        landed(parts[1], block_at(far_row, h), 12 + h)
+        landed(parts[h], block_at(far_row, h), 6 + h)
+        landed(parts[1 - h], block_at(far_row, h), 12 + h)
     turned(row_at(far_row), 2 * owned)
     tab_copy.wait_recv()
     pltpu.sync_copy(tab_v, tab_n)

time: 108 us -> 108 us (level)
  no operation moved by 1% of the time
where the time goes in v8:
time: 108 us; the launch traced here: 106 us
  Pallas kernels  104 us (96%)
  local copies, waits for them, and re-layouts  1.41 us (1%)
  between operations  1.29 us (1%)
    pallas_call x1, Pallas kernels, update(): pl.pallas_call(functools.partial(update_kernel, sites, secs, steps), out_...  104 us

profile of v8, /device:TPU:2, one launch (start us, length us, event | category | flops | bytes accessed | tf_op | source)
XLA Modules:
  0.0 106.5 jit_solution(10190848941165638628)
XLA Ops:
  1.3 103.8 %environments.1 = (bf16[4,2,128,128]{3,2,1,0:T(8,128)(2,1)S(1)}, bf16[4,2,128,128]{3,2,1,0:T(8,128)(2,1)S(1)}) custom-call(s32[4,16]{1,0:T(4,128)} %bitcast.17, s32[4,16]{1,0:T(4,128)} %bitcast.18, f32[1,4]{1,0:T(1,128)} %energy_in.1, f32[1]{0:T(128)S(6)} %copy.13.bond_add, bf16[4,2,128,128]{3,2,1,0:T(8,128)(2,1)} %bitcast.11, ...), custom_call_target="tpu_custom_call" | custom-call | tf_op jit(solution)/shard_map/environments/pallas_call | solution.py:541
  105.1 0.7 copy.14
  105.8 0.7 copy.15

commit v9 on v8

--- a/solution.py
+++ b/solution.py
@@ -59,6 +59,7 @@
 
     barrier = pltpu.get_barrier_semaphore()
     others = [(dy, e) for dy in range(rows) for e in range(2) if (dy, e) != (0, 0)]
+    others.sort(key=lambda at: -min(at[0], rows - at[0]) - at[1])
 
     def sec_of(dy, e):
         other_role = role + e - 2 * role * e

time: 108 us -> 107 us (level)
  no operation moved by 1% of the time
where the time goes in v9:
time: 107 us; the launch traced here: 106 us
  Pallas kernels  103 us (96%)
  local copies, waits for them, and re-layouts  1.41 us (1%)
  between operations  1.29 us (1%)
    pallas_call x1, Pallas kernels, update(): pl.pallas_call(functools.partial(update_kernel, sites, secs, steps), out_...  103 us

profile of v9, /device:TPU:2, one launch (start us, length us, event | category | flops | bytes accessed | tf_op | source)
XLA Modules:
  0.0 105.5 jit_solution(15352009778979930105)
XLA Ops:
  1.3 102.8 %environments.1 = (bf16[4,2,128,128]{3,2,1,0:T(8,128)(2,1)S(1)}, bf16[4,2,128,128]{3,2,1,0:T(8,128)(2,1)S(1)}) custom-call(s32[4,16]{1,0:T(4,128)} %bitcast.17, s32[4,16]{1,0:T(4,128)} %bitcast.18, f32[1,4]{1,0:T(1,128)} %energy_in.1, f32[1]{0:T(128)S(6)} %copy.13.bond_add, bf16[4,2,128,128]{3,2,1,0:T(8,128)(2,1)} %bitcast.11, ...), custom_call_target="tpu_custom_call" | custom-call | tf_op jit(solution)/shard_map/environments/pallas_call | solution.py:542
  104.1 0.7 copy.14
  104.8 0.7 copy.15
